TPU v7x, 32 devices: a whole 2x2x4 slice. The times are simulated.
32 devices in a mesh: vocab: 4 (over y, x), dp: 8 (over z, core).
Axes of the slice: x: 2, y: 2, z: 4, core: 2. Of those that a mesh axis runs over, the one named last changes fastest.
Arguments:
- grads: bfloat16 [4096, 4096], P(('vocab', 'dp')), may hold values from -6 to 6
- token_ids: int32 [4096], P(('vocab', 'dp')), may hold values from 0 to 32063, as said below
Outputs:
- grad_table: float32 [32064, 4096], P('vocab', 'dp')
- row_share: float32 [32064], P('vocab')
Inputs may be any that keep to these rules, and one draw needn't show every extreme that they name: `token_ids`: within the 128 ids of one device (aligned blocks in order) the ids never fall; at most 32 of them lie in the rows k * 8016 to (k + 1) * 8016 - 1 of any one k, and in every block some k has exactly 32.
All inputs are finite; a program needn't handle non-finite values.
Results may differ from a plain program's by a relative error of at most 0.0003.
Values may be sent and summed in bfloat16 or wider, within the bound.
No kernel may reach another device: no remote copies, remote signals or barrier semaphores. Data moves between devices by JAX's collectives and lax.ppermute only.
A program may use at most 64 MiB of HBM per device.

v0:
```python
import math

import jax
import jax.numpy as jnp
from jax import lax
from jax.sharding import PartitionSpec as P

VOCAB_DEV = 8016
TOK_DEV = 128
CAP = 32


def bucket(id_blocks, data_blocks, n_vocab):
    owner_start = jnp.arange(n_vocab, dtype=jnp.int32) * VOCAB_DEV
    starts = jnp.sum((id_blocks[:, None, :] < owner_start[None, :, None]).astype(jnp.int32), axis=2)
    length = id_blocks.shape[1]
    finish = jnp.concatenate(
        [starts[:, 1:], jnp.full((starts.shape[0], 1), length, jnp.int32)], axis=1
    )
    amount = jnp.transpose(finish - starts, (1, 0))
    begins = jnp.transpose(starts, (1, 0))
    slot = jnp.arange(CAP, dtype=jnp.int32)
    places = begins[:, :, None] + slot[None, None, :]
    valid = slot[None, None, :] < amount[:, :, None]
    columns = jnp.arange(length, dtype=jnp.int32)
    select = (places[:, :, :, None] == columns[None, None, None, :]) & valid[:, :, :, None]
    rows = jnp.einsum(
        "vbcl,bld->vbcd",
        select.astype(data_blocks.dtype),
        data_blocks,
        preferred_element_type=jnp.float32,
    )
    rows = rows.astype(data_blocks.dtype).reshape(-1, data_blocks.shape[2])
    picked = jnp.sum(jnp.where(select, id_blocks[None, :, None, :], 0), axis=3)
    slot_ids = jnp.where(valid, picked, -1).reshape(-1)
    return (rows, slot_ids)


def local(grads, token_ids):
    n_vocab = lax.axis_size("vocab")
    n_data = lax.axis_size("dp")
    spread_ids = jnp.broadcast_to(token_ids[:, None], (token_ids.shape[0], n_data))
    split_rows, split_ids = (
        lax.all_to_all(grads, "dp", split_axis=1, concat_axis=0, tiled=True),
        lax.all_to_all(spread_ids, "dp", split_axis=1, concat_axis=0, tiled=True),
    )
    group_ids = split_ids.reshape(n_data, -1)
    group_rows = split_rows.reshape(n_data, group_ids.shape[1], split_rows.shape[1])
    rows, slot_ids = bucket(group_ids, group_rows, n_vocab)
    mine, mine_ids = (
        lax.all_to_all(rows, "vocab", split_axis=0, concat_axis=0, tiled=True),
        lax.all_to_all(slot_ids, "vocab", split_axis=0, concat_axis=0, tiled=True),
    )
    local_rows = jnp.where(mine_ids < 0, -1, mine_ids - lax.axis_index("vocab") * VOCAB_DEV)
    total = local_rows.shape[0]
    width = math.gcd(total, 512)
    row_blocks = mine.reshape(total // width, width, mine.shape[1])
    id_parts = local_rows.reshape(total // width, width)
    table_rows = jnp.arange(VOCAB_DEV, dtype=jnp.int32)

    def accumulate(carry, item):
        table, counts = carry
        block, ids = item
        onehot = ids[:, None] == table_rows[None, :]
        table = table + lax.dot_general(
            onehot.astype(block.dtype),
            block,
            (((0,), (0,)), ((), ())),
            preferred_element_type=jnp.float32,
        )
        counts = counts + jnp.sum(onehot.astype(jnp.float32), axis=0)
        return ((table, counts), None)

    start = (
        jnp.zeros((VOCAB_DEV, mine.shape[1]), jnp.float32),
        jnp.zeros((VOCAB_DEV,), jnp.float32),
    )
    (grad_table, counts), _ = lax.scan(accumulate, start, (row_blocks, id_parts))
    row_share = counts * (VOCAB_DEV / (TOK_DEV * n_data))
    return (grad_table, row_share)


def solution(mesh):
    in_specs = (P(("vocab", "dp"), None), P(("vocab", "dp")))
    out_specs = (P("vocab", "dp"), P("vocab"))
    return jax.shard_map(local, mesh=mesh, in_specs=in_specs, out_specs=out_specs, check_vma=False)
```

profile of v0, /device:TPU:0, one launch (start us, length us, event | category | flops | bytes accessed | tf_op | source)
XLA Modules:
  0.0 92.9 jit_solution(14292049239312270715)
XLA Ops:
  0.6 1.3 %broadcast_in_dim.26 = s32[128,8,1]{0,2,1:T(1,128)} broadcast(s32[128]{0:T(128)} %param.5), dimensions={0} | broadcast | bytes 4608 | tf_op jit(solution)/shard_map/broadcast_in_dim | solution.py:42
  1.9 6.4 %all-to-all-start = ((s32[128,8,1]{0,2,1:T(1,128)}), s32[128,8,1]{0,2,1:T(1,128)S(1)}, u32[]{:S(2)}, u32[]{:S(2)}) async-start(s32[128,8,1]{0,2,1:T(1,128)} %broadcast_in_dim.26), calls=%async_computation | async-start | bytes 8192 | tf_op jit(solution)/shard_map/all_to_all | solution.py:45
  8.2 1.6 %copy.29 = bf16[128,4096]{0,1:T(8,128)(2,1)S(1)} copy(bf16[128,4096]{1,0:T(8,128)(2,1)} %param.4) | data formatting | bytes 2097152 | tf_op args[0]
  9.9 1.3 %copy.30 = bf16[128,8,512]{2,0,1:T(8,128)(2,1)} copy(bf16[128,8,512]{0,2,1:T(8,128)(2,1)S(1)} %bitcast.29) | data formatting | bytes 2097152 | tf_op jit(solution)/shard_map/all_to_all | solution.py:44
  11.2 2.6 %all-to-all-done = s32[128,8,1]{0,2,1:T(1,128)S(1)} async-done(((s32[128,8,1]{0,2,1:T(1,128)}), s32[128,8,1]{0,2,1:T(1,128)S(1)}, u32[]{:S(2)}, u32[]{:S(2)}) %all-to-all-start) | async-done | bytes 4128 | tf_op jit(solution)/shard_map/all_to_all | solution.py:45
  13.7 3.6 %all-to-all-start.2 = ((bf16[128,8,512]{2,0,1:T(8,128)(2,1)}), bf16[128,8,512]{2,0,1:T(8,128)(2,1)S(1)}, u32[]{:S(2)}, u32[]{:S(2)}) async-start(bf16[128,8,512]{2,0,1:T(8,128)(2,1)} %copy.30), calls=%async_computation.2 | async-start | bytes 2097152 | tf_op jit(solution)/shard_map/all_to_all | solution.py:44
  17.4 0.2 convert_reduce_fusion
  17.7 0.1 copy.23
  17.9 0.9 select_reduce_fusion
  19.0 0.1 lt.58
  19.1 0.6 copy.26
  19.7 24.1 %all-to-all-done.2 = bf16[128,8,512]{2,0,1:T(8,128)(2,1)S(1)} async-done(((bf16[128,8,512]{2,0,1:T(8,128)(2,1)}), bf16[128,8,512]{2,0,1:T(8,128)(2,1)S(1)}, u32[]{:S(2)}, u32[]{:S(2)}) %all-to-all-start.2) | async-done | bytes 1048608 | tf_op jit(solution)/shard_map/all_to_all | solution.py:44
  43.8 3.7 %all-to-all-start.1 = ((s32[4,256,1]{1,2,0:T(1,128)}), s32[4,256,1]{1,2,0:T(1,128)S(1)}, u32[]{:S(2)}, u32[]{:S(2)}) async-start(s32[4,256,1]{1,2,0:T(1,128)} %copy.26), calls=%async_computation.1 | async-start | bytes 8192 | tf_op jit(solution)/shard_map/all_to_all | solution.py:52
  47.5 0.5 fusion.9
  48.0 1.1 %copy.31 = bf16[4,8,32,512]{3,2,1,0:T(8,128)(2,1)} copy(bf16[4,8,32,512]{3,2,0,1:T(8,128)(2,1)S(1)} %fusion.9) | data formatting | bytes 2097152 | tf_op jit(solution)/shard_map/convert_element_type | solution.py:33
  49.1 3.1 %all-to-all-done.1 = s32[4,256,1]{1,2,0:T(1,128)S(1)} async-done(((s32[4,256,1]{1,2,0:T(1,128)}), s32[4,256,1]{1,2,0:T(1,128)S(1)}, u32[]{:S(2)}, u32[]{:S(2)}) %all-to-all-start.1) | async-done | bytes 4128 | tf_op jit(solution)/shard_map/all_to_all | solution.py:52
  52.2 3.5 %all-to-all-start.3 = ((bf16[4,256,512]{2,1,0:T(8,128)(2,1)}), bf16[4,256,512]{2,1,0:T(8,128)(2,1)S(1)}, u32[]{:S(2)}, u32[]{:S(2)}) async-start(bf16[4,256,512]{2,1,0:T(8,128)(2,1)} %bitcast.10), calls=%async_computation.3 | async-start | bytes 2097152 | tf_op jit(solution)/shard_map/all_to_all | solution.py:51
  55.8 12.1 %all-to-all-done.3 = bf16[4,256,512]{2,1,0:T(8,128)(2,1)S(1)} async-done(((bf16[4,256,512]{2,1,0:T(8,128)(2,1)}), bf16[4,256,512]{2,1,0:T(8,128)(2,1)S(1)}, u32[]{:S(2)}, u32[]{:S(2)}) %all-to-all-start.3) | async-done | bytes 1048608 | tf_op jit(solution)/shard_map/all_to_all | solution.py:51
  67.9 24.4 %while.13 = (s32[]{:T(128)}, f32[8016,512]{1,0:T(8,128)}, f32[8016]{0:T(1024)S(1)}, s32[2,512]{1,0:T(2,128)S(1)}, bf16[2,512,512]{2,1,0:T(8,128)(2,1)S(1)}, /*index=5*/s32[]{:T(128)}, s32[]{:T(128)}) while((s32[]{:T(128)}, f32[8016,512]{1,0:T(8,128)}, f32[8016]{0:T(1024)S(1)}, s32[2,512]{1,0:T(2,128)S(1)}, ...), condition=%wide.region_4.5_spmd.clone, body=%wide.region_2.4_spmd.clone.sunk | while | flops 4227325952 | bytes 33494372 | solution.py:78
  67.9 1.8 %fusion.18 = f32[8016]{0:T(1024)S(1)} fusion(s32[512]{0:T(512)S(1)} %bitcast.30), kind=kLoop, calls=%fused_computation.4.clone.1 | loop fusion | flops 12304560 | bytes 34112 | tf_op jit(solution)/shard_map/while/body/eval_jaxpr/reduce_sum | solution.py:71
  69.7 8.7 %select_add_fusion.4 = f32[8016,512]{1,0:T(8,128)} fusion(f32[8016,512]{1,0:T(8,128)} %get-tuple-element.106, s32[512]{0:T(512)S(1)} %bitcast.31, pred[]{:T(512)S(6)} %compare.4, bf16[2,512,512]{2,1,0:T(8,128)(2,1)S(1)} %get-tuple-element.116, s32[]{:T(128)S(6)} %copy.37), kind=kOutput, calls=%fused_computation.5.clone.1 | convolution fusion | flops 4215005184 | bytes 33359876 | tf_op jit(solution)/shard_map/while/body/eval_jaxpr/dot_general | solution.py:65
  78.4 1.8 %fusion.18 = f32[8016]{0:T(1024)S(1)} fusion(s32[512]{0:T(512)S(1)} %bitcast.30), kind=kLoop, calls=%fused_computation.4.clone.1 | loop fusion | flops 12304560 | bytes 34112 | tf_op jit(solution)/shard_map/while/body/eval_jaxpr/reduce_sum | solution.py:71
  80.3 12.0 %select_add_fusion.4 = f32[8016,512]{1,0:T(8,128)} fusion(f32[8016,512]{1,0:T(8,128)} %get-tuple-element.106, s32[512]{0:T(512)S(1)} %bitcast.31, pred[]{:T(512)S(6)} %compare.4, bf16[2,512,512]{2,1,0:T(8,128)(2,1)S(1)} %get-tuple-element.116, s32[]{:T(128)S(6)} %copy.37), kind=kOutput, calls=%fused_computation.5.clone.1 | convolution fusion | flops 4215005184 | bytes 33359876 | tf_op jit(solution)/shard_map/while/body/eval_jaxpr/dot_general | solution.py:65
  92.3 0.6 broadcast_multiply_fusion
  (20 shorter events, 0.5 us)
Async XLA Ops:
  1.9 11.9 %all-to-all-start = ((s32[128,8,1]{0,2,1:T(1,128)}), s32[128,8,1]{0,2,1:T(1,128)S(1)}, u32[]{:S(2)}, u32[]{:S(2)}) async-start(s32[128,8,1]{0,2,1:T(1,128)} %broadcast_in_dim.26), calls=%async_computation | async-start | bytes 8192 | tf_op jit(solution)/shard_map/all_to_all | solution.py:45
  13.7 30.1 %all-to-all-start.2 = ((bf16[128,8,512]{2,0,1:T(8,128)(2,1)}), bf16[128,8,512]{2,0,1:T(8,128)(2,1)S(1)}, u32[]{:S(2)}, u32[]{:S(2)}) async-start(bf16[128,8,512]{2,0,1:T(8,128)(2,1)} %copy.30), calls=%async_computation.2 | async-start | bytes 2097152 | tf_op jit(solution)/shard_map/all_to_all | solution.py:44
  43.8 8.4 %all-to-all-start.1 = ((s32[4,256,1]{1,2,0:T(1,128)}), s32[4,256,1]{1,2,0:T(1,128)S(1)}, u32[]{:S(2)}, u32[]{:S(2)}) async-start(s32[4,256,1]{1,2,0:T(1,128)} %copy.26), calls=%async_computation.1 | async-start | bytes 8192 | tf_op jit(solution)/shard_map/all_to_all | solution.py:52
  52.2 15.7 %all-to-all-start.3 = ((bf16[4,256,512]{2,1,0:T(8,128)(2,1)}), bf16[4,256,512]{2,1,0:T(8,128)(2,1)S(1)}, u32[]{:S(2)}, u32[]{:S(2)}) async-start(bf16[4,256,512]{2,1,0:T(8,128)(2,1)} %bitcast.10), calls=%async_computation.3 | async-start | bytes 2097152 | tf_op jit(solution)/shard_map/all_to_all | solution.py:51
where the time goes:
time: 93.3 us; the launch traced here: 92.9 us
  waiting for transfers between devices  41.9 us (45%)
  matrix products  21.2 us (23%)
  starting transfers between devices  17.1 us (18%)
  local copies, waits for them, and re-layouts  6.29 us (7%)
  other arithmetic  5.63 us (6%)
    all_to_all x1, waiting for transfers between devices, local(): lax.all_to_all(grads, 'dp', split_axis=1, concat_axis=0, tiled=True)  24.1 us
    dot_general x2, matrix products, accumulate(): lax.dot_general(onehot.astype(block.dtype), block, (((0,), (0,)), ((), ()...  20.7 us
    all_to_all x1, waiting for transfers between devices, local(): lax.all_to_all(rows, 'vocab', split_axis=0, concat_axis=0, tiled=True)  12.1 us
    all_to_all x1, starting transfers between devices, local(): lax.all_to_all(spread_ids, 'dp', split_axis=1, concat_axis=0, tiled=True)  6.35 us
    all_to_all x1, starting transfers between devices, local(): lax.all_to_all(slot_ids, 'vocab', split_axis=0, concat_axis=0, tiled=True)  3.72 us
    reduce_sum x2, other arithmetic, accumulate(): counts = counts + jnp.sum(onehot.astype(jnp.float32), axis=0)  3.68 us
    all_to_all x1, starting transfers between devices, local(): lax.all_to_all(grads, 'dp', split_axis=1, concat_axis=0, tiled=True)  3.56 us
    all_to_all x1, starting transfers between devices, local(): lax.all_to_all(rows, 'vocab', split_axis=0, concat_axis=0, tiled=True)  3.52 us
  transfers between devices with their start and end apart: 4, of which 4 were waited for; matrix products, arithmetic and copies ran while one was open for 7% of the time, Pallas kernels for 0%

commit v1 on v0

v1 whole, which is shorter than its diff:
```python
import jax
import jax.numpy as jnp
from jax import lax
from jax.sharding import PartitionSpec as P

VOCAB_DEV = 8016
TOK_DEV = 128
CAP = 32
AXES = ("vocab", "dp")


def bucket(ids, data, n_vocab):
    owner_start = jnp.arange(n_vocab, dtype=jnp.int32) * VOCAB_DEV
    length = ids.shape[0]
    if n_vocab * CAP == length:
        return data, ids.reshape(n_vocab, CAP) - owner_start[:, None]
    starts = jnp.sum((ids[None, :] < owner_start[:, None]).astype(jnp.int32), axis=1)
    finish = jnp.concatenate([starts[1:], jnp.full((1,), length, jnp.int32)])
    slot = jnp.arange(CAP, dtype=jnp.int32)
    places = starts[:, None] + slot[None, :]
    valid = places < finish[:, None]
    columns = jnp.arange(length, dtype=jnp.int32)
    select = (places[:, :, None] == columns) & valid[:, :, None]
    rows = jnp.einsum(
        "vcl,ld->vcd", select.astype(data.dtype), data, preferred_element_type=jnp.float32
    ).astype(data.dtype)
    picked = jnp.sum(jnp.where(select, ids, 0), axis=2)
    slot_ids = jnp.where(valid, picked - owner_start[:, None], -1)
    return rows.reshape(n_vocab * CAP, data.shape[1]), slot_ids


def local(grads, token_ids):
    n_vocab = lax.axis_size("vocab")
    n_data = lax.axis_size("dp")
    width = grads.shape[1] // n_data
    rows, slot_ids = bucket(token_ids, grads, n_vocab)
    rows = rows.reshape(n_vocab, CAP, n_data, width).transpose(0, 2, 1, 3)
    rows = rows.reshape(n_vocab * n_data, CAP, width)
    slot_ids = jnp.broadcast_to(slot_ids[:, None, :], (n_vocab, n_data, CAP)).reshape(n_vocab * n_data, CAP)
    mine = lax.all_to_all(rows, AXES, split_axis=0, concat_axis=0, tiled=True)
    mine_ids = lax.all_to_all(slot_ids, AXES, split_axis=0, concat_axis=0, tiled=True)
    mine = mine.reshape(-1, width)
    mine_ids = mine_ids.reshape(-1)
    table_rows = jnp.arange(VOCAB_DEV, dtype=jnp.int32)
    onehot = table_rows[:, None] == mine_ids[None, :]
    table = lax.dot_general(
        onehot.astype(mine.dtype), mine, (((1,), (0,)), ((), ())), preferred_element_type=jnp.float32
    )
    counts = jnp.sum(onehot.astype(jnp.float32), axis=1)
    return table, counts * (VOCAB_DEV / (TOK_DEV * n_data))


def solution(mesh):
    in_specs = (P(AXES, None), P(AXES))
    out_specs = (P("vocab", "dp"), P("vocab"))
    return jax.shard_map(local, mesh=mesh, in_specs=in_specs, out_specs=out_specs, check_vma=False)
```

time: 93.3 us -> 58.4 us (0.63)
  waiting for transfers between devices: 41.9 us -> 26.2 us
  matrix products: 21.2 us -> 11.5 us
  starting transfers between devices: 17.1 us -> 9.97 us
  local copies, waits for them, and re-layouts: 6.29 us -> 4.92 us
    all_to_all x4 -> x2, waiting for transfers between devices: 41.9 us -> 26.2 us  [the longest x1 22.1 us: local(): mine = lax.all_to_all(rows, AXES, split_axis=0, concat_axis=0, tiled=True)]
    dot_general x3 -> x1, matrix products: 21.2 us -> 11.5 us  [local(): lax.dot_general(onehot.astype(mine.dtype), mine, (((1,), (0,)), ((), ()))...]
    all_to_all x4 -> x2, starting transfers between devices: 17.1 us -> 9.97 us  [the longest x1 7.33 us: local(): lax.all_to_all(slot_ids, AXES, split_axis=0, concat_axis=0, tiled=True)]
    reduce_sum x4 -> x1, other arithmetic: 4.82 us -> 3.42 us  [local(): counts = jnp.sum(onehot.astype(jnp.float32), axis=1)]
    transpose x1 -> x2, local copies, waits for them, and re-layouts: 0.08 us -> 1.37 us  [local(): rows = rows.reshape(n_vocab, CAP, n_data, width).transpose(0, 2, 1, 3)]
    convert_element_type x1 -> x0, local copies, waits for them, and re-layouts: 1.06 us -> none  [bucket(): rows = rows.astype(data_blocks.dtype).reshape(-1, data_blocks.shape[2])]
  transfers between devices with their start and end apart: 4 -> 2, of which waited for: 4 -> 2; matrix products, arithmetic and copies ran while one was open for 7% -> 14% of each run, Pallas kernels for 0% -> 0%
where the time goes in v1:
time: 58.4 us; the launch traced here: 58.1 us
  waiting for transfers between devices  26.2 us (45%)
  matrix products  11.5 us (20%)
  starting transfers between devices  9.97 us (17%)
  local copies, waits for them, and re-layouts  4.92 us (8%)
  other arithmetic  4.81 us (8%)
  between operations  0.67 us (1%)
    all_to_all x1, waiting for transfers between devices, local(): mine = lax.all_to_all(rows, AXES, split_axis=0, concat_axis=0, tiled=True)  22.1 us
    dot_general x1, matrix products, local(): lax.dot_general(onehot.astype(mine.dtype), mine, (((1,), (0,)), ((), ()))...  11.5 us
    all_to_all x1, starting transfers between devices, local(): lax.all_to_all(slot_ids, AXES, split_axis=0, concat_axis=0, tiled=True)  7.33 us
    all_to_all x1, waiting for transfers between devices, local(): lax.all_to_all(slot_ids, AXES, split_axis=0, concat_axis=0, tiled=True)  4.1 us
    reduce_sum x1, other arithmetic, local(): counts = jnp.sum(onehot.astype(jnp.float32), axis=1)  3.42 us
    all_to_all x1, starting transfers between devices, local(): mine = lax.all_to_all(rows, AXES, split_axis=0, concat_axis=0, tiled=True)  2.65 us
    unnamed x1, local copies, waits for them, and re-layouts  1.62 us
    transpose x2, local copies, waits for them, and re-layouts, local(): rows = rows.reshape(n_vocab, CAP, n_data, width).transpose(0, 2, 1, 3)  1.37 us
  transfers between devices with their start and end apart: 2, of which 2 were waited for; matrix products, arithmetic and copies ran while one was open for 14% of the time, Pallas kernels for 0%

profile of v1, /device:TPU:0, one launch (start us, length us, event | category | flops | bytes accessed | tf_op | source)
XLA Modules:
  0.0 58.1 jit_solution(4642271783880654018)
XLA Ops:
  0.6 0.7 %reshape.42 = s32[4,32]{1,0:T(4,128)S(1)} reshape(s32[128]{0:T(128)} %param.3) | data formatting | bytes 1024 | tf_op jit(solution)/shard_map/reshape | solution.py:16
  1.4 0.1 broadcast_subtract_fusion
  1.5 0.6 %broadcast_in_dim.2 = s32[4,8,32]{2,1,0:T(8,128)} broadcast(s32[4,32]{1,0:T(4,128)S(1)} %broadcast_subtract_fusion), dimensions={0,2} | broadcast | bytes 4608 | tf_op jit(solution)/shard_map/broadcast_in_dim | solution.py:39
  2.1 7.3 %all-to-all-start = ((s32[32,1,32]{2,1,0:T(1,128)}), s32[32,1,32]{2,1,0:T(1,128)S(1)}, u32[]{:S(2)}, u32[]{:S(2)}) async-start(s32[32,1,32]{2,1,0:T(1,128)} %bitcast), calls=%async_computation | async-start | bytes 32768 | tf_op jit(solution)/shard_map/all_to_all | solution.py:41
  9.4 1.6 %copy.7 = bf16[16,8,8,512]{3,2,1,0:T(8,128)(2,1)S(1)} copy(bf16[16,8,8,512]{3,1,2,0:T(8,128)(2,1)} %bitcast.12) | data formatting | bytes 2097152
  11.0 0.1 bitcast_bitcast_fusion
  11.1 1.3 %copy.6 = bf16[4,8,32,512]{3,2,1,0:T(8,128)(2,1)} copy(bf16[4,8,32,512]{3,1,2,0:T(8,128)(2,1)S(1)} %bitcast_bitcast_fusion) | data formatting | bytes 2097152 | tf_op jit(solution)/shard_map/transpose | solution.py:37
  12.4 4.1 %all-to-all-done = s32[32,1,32]{2,1,0:T(1,128)S(1)} async-done(((s32[32,1,32]{2,1,0:T(1,128)}), s32[32,1,32]{2,1,0:T(1,128)S(1)}, u32[]{:S(2)}, u32[]{:S(2)}) %all-to-all-start) | async-done | bytes 4128 | tf_op jit(solution)/shard_map/all_to_all | solution.py:41
  16.5 2.6 %all-to-all-start.1 = ((bf16[32,32,512]{2,1,0:T(8,128)(2,1)}), bf16[32,32,512]{2,1,0:T(8,128)(2,1)S(1)}, u32[]{:S(2)}, u32[]{:S(2)}) async-start(bf16[32,32,512]{2,1,0:T(8,128)(2,1)} %bitcast.2), calls=%async_computation.1 | async-start | bytes 2097152 | tf_op jit(solution)/shard_map/all_to_all | solution.py:40
  19.1 0.5 broadcast.20
  19.7 0.7 %reduce.3 = s32[32,32]{1,0:T(8,128)S(1)} reduce(s32[32,1,32]{2,1,0:T(1,128)S(1)} %all-to-all-done, s32[]{:T(128)} %broadcast.20), dimensions={1}, to_apply=%all_to_all.10.reduce_sub_computation.3 | reduce | bytes 8196 | tf_op jit(solution)/shard_map/all_to_all | solution.py:41
  20.4 0.1 eq.16
  20.4 3.4 %convert_reduce_fusion = f32[8016]{0:T(1024)S(1)} fusion(s32[1024]{0:T(1024)S(1)} %eq.16), kind=kLoop, calls=%fused_computation | loop fusion | flops 24617136 | bytes 36160 | tf_op jit(solution)/shard_map/reduce_sum | solution.py:49
  23.9 0.6 %broadcast_multiply_fusion = f32[8016]{0:T(1024)} fusion(f32[8016]{0:T(1024)S(1)} %convert_reduce_fusion), kind=kLoop, calls=%fused_computation.5 | loop fusion | flops 8016 | bytes 64128 | tf_op jit(solution)/shard_map/mul | solution.py:50
  24.5 22.1 %all-to-all-done.1 = bf16[32,32,512]{2,1,0:T(8,128)(2,1)S(1)} async-done(((bf16[32,32,512]{2,1,0:T(8,128)(2,1)}), bf16[32,32,512]{2,1,0:T(8,128)(2,1)S(1)}, u32[]{:S(2)}, u32[]{:S(2)}) %all-to-all-start.1) | async-done | bytes 1048608 | tf_op jit(solution)/shard_map/all_to_all | solution.py:40
  46.6 11.5 %fusion = f32[8016,512]{1,0:T(8,128)} fusion(bf16[1024,512]{1,0:T(8,128)(2,1)S(1)} %bitcast.13, s32[1024]{0:T(1024)S(1)} %eq.16), kind=kOutput, calls=%fused_computation.2 | convolution fusion | flops 8413593600 | bytes 17469440 | tf_op jit(solution)/shard_map/dot_general | solution.py:46
  (1 shorter events, 0.0 us)
Async XLA Ops:
  2.1 14.4 %all-to-all-start = ((s32[32,1,32]{2,1,0:T(1,128)}), s32[32,1,32]{2,1,0:T(1,128)S(1)}, u32[]{:S(2)}, u32[]{:S(2)}) async-start(s32[32,1,32]{2,1,0:T(1,128)} %bitcast), calls=%async_computation | async-start | bytes 32768 | tf_op jit(solution)/shard_map/all_to_all | solution.py:41
  16.5 30.1 %all-to-all-start.1 = ((bf16[32,32,512]{2,1,0:T(8,128)(2,1)}), bf16[32,32,512]{2,1,0:T(8,128)(2,1)S(1)}, u32[]{:S(2)}, u32[]{:S(2)}) async-start(bf16[32,32,512]{2,1,0:T(8,128)(2,1)} %bitcast.2), calls=%async_computation.1 | async-start | bytes 2097152 | tf_op jit(solution)/shard_map/all_to_all | solution.py:40

commit v2 on v1

v2 whole, which is shorter than its diff:
```python
import functools

import jax
import jax.numpy as jnp
from jax import lax
from jax.experimental import pallas as pl
from jax.experimental.pallas import tpu as pltpu
from jax.sharding import PartitionSpec as P

VOCAB_DEV = 8016
TOK_DEV = 128
CAP = 32
AXES = ("vocab", "dp")
LANES = 128
GROUP = LANES // CAP
ID_ROWS = 8
BLOCK = 512
PAIR = 2
BLOCKS = -(-VOCAB_DEV // (BLOCK * PAIR)) * PAIR
WINDOW = 256


def bucket(ids, data, n_vocab):
    length = ids.shape[0]
    if n_vocab * CAP == length:
        return data, ids.reshape(1, length)
    owner_start = jnp.arange(n_vocab, dtype=jnp.int32) * VOCAB_DEV
    starts = jnp.sum((ids[None, :] < owner_start[:, None]).astype(jnp.int32), axis=1)
    finish = jnp.concatenate([starts[1:], jnp.full((1,), length, jnp.int32)])
    slot = jnp.arange(CAP, dtype=jnp.int32)
    places = starts[:, None] + slot[None, :]
    valid = places < finish[:, None]
    columns = jnp.arange(length, dtype=jnp.int32)
    select = (places[:, :, None] == columns) & valid[:, :, None]
    rows = jnp.einsum(
        "vcl,ld->vcd", select.astype(data.dtype), data, preferred_element_type=jnp.float32
    ).astype(data.dtype)
    picked = jnp.sum(jnp.where(select, ids, 0), axis=2)
    slot_ids = jnp.where(valid, picked, -1)
    return rows.reshape(n_vocab * CAP, data.shape[1]), slot_ids.reshape(1, n_vocab * CAP)


def pack_kernel(n_vocab, n_data, rows_hbm, ids_ref, out_hbm, rows, out, in_sem, out_sem):
    tiles = rows.shape[1] // (n_data * LANES)
    loads = []
    for v in range(n_vocab):
        strip = pl.ds(v * CAP, CAP)
        loads.append(pltpu.make_async_copy(rows_hbm.at[strip], rows.at[strip], in_sem.at[v]))
        loads[-1].start()
    source = lax.axis_index("vocab") * n_data + lax.axis_index("dp")
    lane = lax.broadcasted_iota(jnp.int32, (ID_ROWS, LANES), 1)
    sub = lax.broadcasted_iota(jnp.int32, (ID_ROWS, LANES), 0)
    row = lax.rem(lax.div(source, GROUP), ID_ROWS // 2)
    here = lax.div(lane, CAP) == lax.rem(source, GROUP)
    stores = []
    for v in range(n_vocab):
        ids = ids_ref[:, v * CAP : (v + 1) * CAP]
        ids = jnp.where(ids < 0, -1, ids - v * VOCAB_DEV)
        ids = jnp.concatenate([ids] * GROUP, axis=1)
        high = lax.shift_right_arithmetic(ids, 7).astype(jnp.float32)
        low = jnp.bitwise_and(ids, 127).astype(jnp.float32)
        coded = jnp.where(here & (sub == row), high, 0.0) + jnp.where(here & (sub == row + ID_ROWS // 2), low, 0.0)
        coded = coded.astype(out.dtype)
        loads[v].wait()
        for d in range(n_data):
            for j in range(tiles):
                column = (d * tiles + j) * LANES
                out[v * n_data + d, j * CAP : (j + 1) * CAP, :] = rows[
                    v * CAP : (v + 1) * CAP, column : column + LANES
                ]
            out[v * n_data + d, tiles * CAP : tiles * CAP + ID_ROWS, :] = coded
        strip = pl.ds(v * n_data, n_data)
        stores.append(pltpu.make_async_copy(out.at[strip], out_hbm.at[strip], out_sem.at[v]))
        stores[-1].start()
    for store in stores:
        store.wait()


def pack(rows, ids, n_vocab, n_data):
    width = rows.shape[1] // n_data
    length = width // LANES * CAP + ID_ROWS
    shape = (n_vocab * n_data, length, LANES)
    return pl.pallas_call(
        functools.partial(pack_kernel, n_vocab, n_data),
        out_shape=jax.ShapeDtypeStruct(shape, rows.dtype),
        in_specs=[pl.BlockSpec(memory_space=pl.ANY), pl.BlockSpec(memory_space=pltpu.VMEM)],
        out_specs=pl.BlockSpec(memory_space=pl.ANY),
        scratch_shapes=[
            pltpu.VMEM(rows.shape, rows.dtype),
            pltpu.VMEM(shape, rows.dtype),
            pltpu.SemaphoreType.DMA((n_vocab,)),
            pltpu.SemaphoreType.DMA((n_vocab,)),
        ],
        name="pack",
    )(rows, ids)


def table_kernel(
    scale, got, table_hbm, share_ref, x, ids_s, key_s, column_s, rank_s, sorted_ids, sorted_columns, sorted_x, table, starts, sem
):
    sources, length, _ = got.shape
    total = sources * CAP
    chunks = total // LANES
    tiles = (length - ID_ROWS) // CAP
    half = ID_ROWS // 2
    per = half * GROUP
    for g in range(sources // per):
        coded = got[g * per, tiles * CAP :, :].astype(jnp.float32)
        for s in range(g * per + 1, (g + 1) * per):
            coded = coded + got[s, tiles * CAP :, :].astype(jnp.float32)
        ids_s[g * half : (g + 1) * half, :] = (coded[:half] * 128.0 + coded[half:]).astype(jnp.int32)
    ids = ids_s[...]
    ids = jnp.where(ids < 0, BLOCKS * BLOCK, ids)
    token = lax.broadcasted_iota(jnp.int32, (chunks, LANES), 0) * LANES + lax.broadcasted_iota(
        jnp.int32, (chunks, LANES), 1
    )
    key = ids * total + token
    key_s[...] = key
    turned = key.T
    for q in range(chunks):
        column_s[q * LANES : (q + 1) * LANES, :] = jnp.broadcast_to(turned[:, q : q + 1], (LANES, LANES))
    for b in range(BLOCKS + 1):
        starts[b] = jnp.sum((ids < b * BLOCK).astype(jnp.int32))
    for j in range(tiles):
        x[:, j * LANES : (j + 1) * LANES] = got[:, j * CAP : (j + 1) * CAP, :].reshape(total, LANES)

    def count(q, before):
        column = column_s[pl.ds(pl.multiple_of(q * LANES, LANES), LANES), :].reshape(LANES // 8, 8, LANES)
        return tuple(
            before[p] + jnp.sum((column < key_s[p : p + 1, :].reshape(1, 1, LANES)).astype(jnp.int32), axis=0)
            for p in range(chunks)
        )

    before = lax.fori_loop(0, chunks, count, tuple(jnp.zeros((8, LANES), jnp.int32) for _ in range(chunks)))
    for p in range(chunks):
        rank_s[p : p + 1, :] = jnp.sum(before[p], axis=0, keepdims=True)

    flat = jnp.concatenate([ids[p : p + 1, :] for p in range(chunks)], axis=1)
    pick = lax.broadcasted_iota(jnp.int32, (8, total), 0)
    parts = jnp.where(pick == 0, lax.shift_right_arithmetic(flat, 7), jnp.bitwise_and(flat, 127))
    parts = parts.astype(jnp.float32).astype(x.dtype)

    def order(c, _):
        place = lax.broadcasted_iota(jnp.int32, (WINDOW, LANES), 0) + c * WINDOW
        move = jnp.concatenate(
            [jnp.where(rank_s[p : p + 1, :] == place, 1.0, 0.0).astype(x.dtype) for p in range(chunks)], axis=1
        )
        at = pl.ds(pl.multiple_of(c * WINDOW, WINDOW), WINDOW)
        sorted_x[at, :] = jnp.dot(move, x[...], preferred_element_type=jnp.float32).astype(x.dtype)
        moved = lax.dot_general(parts, move, (((1,), (1,)), ((), ())), preferred_element_type=jnp.float32)
        moved = (moved[0:1] * 128.0 + moved[1:2]).astype(jnp.int32)
        for i in range(WINDOW // LANES):
            sorted_ids[pl.ds(c * (WINDOW // LANES) + i, 1), :] = moved[:, i * LANES : (i + 1) * LANES]
        return 0

    lax.fori_loop(0, total // WINDOW, order, 0)
    sorted_ids[chunks : chunks + 8, :] = jnp.full((8, LANES), -1, jnp.int32)
    sorted_x[total : total + LANES, :] = jnp.zeros((LANES, x.shape[1]), x.dtype)
    turned = sorted_ids[...].T
    for q in range(chunks + 1):
        sorted_columns[q * LANES : (q + 1) * LANES, :] = jnp.broadcast_to(turned[:, q : q + 1], (LANES, LANES))

    def rows_of(b, k):
        place = lax.broadcasted_iota(jnp.int32, (BLOCK, LANES), 0) + b * BLOCK
        hit = jnp.concatenate(
            [
                jnp.where(sorted_ids[pl.ds(k + i, 1), :] == place, 1.0, 0.0).astype(x.dtype)
                for i in range(WINDOW // LANES)
            ],
            axis=1,
        )
        at = pl.ds(pl.multiple_of(k * LANES, LANES), WINDOW)
        return jnp.dot(hit, sorted_x[at, :], preferred_element_type=jnp.float32)

    def counts_of(b, k):
        column = sorted_columns[pl.ds(pl.multiple_of(k * LANES, LANES), WINDOW), :].reshape(WINDOW // 8, 8, LANES)
        place = lax.broadcasted_iota(jnp.int32, (1, 1, LANES), 2) + b * BLOCK
        return jnp.concatenate(
            [
                jnp.sum(jnp.sum((column == place + i * LANES).astype(jnp.float32), axis=0), axis=0, keepdims=True)
                for i in range(BLOCK // LANES)
            ],
            axis=0,
        )

    last = BLOCKS - 1
    rest = VOCAB_DEV - last * BLOCK

    def out_copy(b, n):
        at = pl.ds(pl.multiple_of(b * BLOCK, BLOCK), n)
        return pltpu.make_async_copy(table.at[at, :], table_hbm.at[at, :], sem.at[b])

    def build(step, _):
        for i in range(PAIR):
            b = step * PAIR + i
            k = jnp.minimum(lax.shift_right_logical(starts[b], 7), chunks - 1)
            table[pl.ds(pl.multiple_of(b * BLOCK, BLOCK), BLOCK), :] = rows_of(b, k)
            share_ref[pl.ds(b * (BLOCK // LANES), BLOCK // LANES), :] = counts_of(b, k) * scale
        for i in range(PAIR):
            b = step * PAIR + i
            k = jnp.minimum(lax.shift_right_logical(starts[b], 7), chunks - 1)
            more = lax.div(jnp.maximum(starts[b + 1] - k * LANES - 1, 0), WINDOW)

            def further(w, _, b=b, k=k):
                at = pl.ds(pl.multiple_of(b * BLOCK, BLOCK), BLOCK)
                table[at, :] += rows_of(b, k + w * (WINDOW // LANES))
                at = pl.ds(b * (BLOCK // LANES), BLOCK // LANES)
                share_ref[at, :] += counts_of(b, k + w * (WINDOW // LANES)) * scale
                return 0

            lax.fori_loop(1, more + 1, further, 0)

            @pl.when(b < last)
            def _(b=b):
                out_copy(b, BLOCK).start()

            @pl.when(b == last)
            def _():
                out_copy(last, rest).start()

        return 0

    lax.fori_loop(0, BLOCKS // PAIR, build, 0)
    for b in range(last):
        out_copy(b, BLOCK).wait()
    out_copy(last, rest).wait()


def make_table(got, scale):
    sources, length, _ = got.shape
    total = sources * CAP
    chunks = total // LANES
    width = (length - ID_ROWS) // CAP * LANES
    return pl.pallas_call(
        functools.partial(table_kernel, scale),
        out_shape=(
            jax.ShapeDtypeStruct((VOCAB_DEV, width), jnp.float32),
            jax.ShapeDtypeStruct((BLOCKS * BLOCK // LANES, LANES), jnp.float32),
        ),
        in_specs=[pl.BlockSpec(memory_space=pltpu.VMEM)],
        out_specs=(pl.BlockSpec(memory_space=pl.ANY), pl.BlockSpec(memory_space=pltpu.VMEM)),
        scratch_shapes=[
            pltpu.VMEM((total, width), got.dtype),
            pltpu.VMEM((chunks, LANES), jnp.int32),
            pltpu.VMEM((chunks, LANES), jnp.int32),
            pltpu.VMEM((total, LANES), jnp.int32),
            pltpu.VMEM((chunks, LANES), jnp.int32),
            pltpu.VMEM((chunks + 8, LANES), jnp.int32),
            pltpu.VMEM((total + LANES, LANES), jnp.int32),
            pltpu.VMEM((total + LANES, width), got.dtype),
            pltpu.VMEM((BLOCKS * BLOCK, width), jnp.float32),
            pltpu.SMEM((BLOCKS + 1,), jnp.int32),
            pltpu.SemaphoreType.DMA((BLOCKS,)),
        ],
        compiler_params=pltpu.CompilerParams(vmem_limit_bytes=48 * 1024 * 1024),
        name="table",
    )(got)


def local(grads, token_ids):
    n_vocab = lax.axis_size("vocab")
    n_data = lax.axis_size("dp")
    rows, ids = bucket(token_ids, grads, n_vocab)
    sent = pack(rows, ids, n_vocab, n_data)
    got = lax.all_to_all(sent, AXES, split_axis=0, concat_axis=0, tiled=True)
    table, share = make_table(got, VOCAB_DEV / (TOK_DEV * n_data))
    return table, share.reshape(-1)[:VOCAB_DEV]


def solution(mesh):
    in_specs = (P(AXES, None), P(AXES))
    out_specs = (P("vocab", "dp"), P("vocab"))
    return jax.shard_map(local, mesh=mesh, in_specs=in_specs, out_specs=out_specs, check_vma=False)
```

time: 58.4 us -> 50.5 us (0.86)
  blocking collectives: 0 us -> 36.5 us
  waiting for transfers between devices: 26.2 us -> 0 us
  Pallas kernels: 0 us -> 13.1 us
  matrix products: 11.5 us -> 0 us
  starting transfers between devices: 9.97 us -> 0 us
  local copies, waits for them, and re-layouts: 4.92 us -> 0 us
  other arithmetic: 4.81 us -> 0 us
    all_to_all x0 -> x1, blocking collectives: none -> 36.5 us  [local(): got = lax.all_to_all(sent, AXES, split_axis=0, concat_axis=0, tiled=True)]
    all_to_all x2 -> x0, waiting for transfers between devices: 26.2 us -> none  [the longest x1 22.1 us: local(): mine = lax.all_to_all(rows, AXES, split_axis=0, concat_axis=0, tiled=True)]
    pallas_call x0 -> x2, Pallas kernels: none -> 13.1 us  [the longest x1 10.4 us: make_table(): pl.pallas_call(functools.partial(table_kernel, scale), out_shape=(jax.Sha...]
    dot_general x1 -> x0, matrix products: 11.5 us -> none  [local(): lax.dot_general(onehot.astype(mine.dtype), mine, (((1,), (0,)), ((), ()))...]
    all_to_all x2 -> x0, starting transfers between devices: 9.97 us -> none  [the longest x1 7.33 us: local(): lax.all_to_all(slot_ids, AXES, split_axis=0, concat_axis=0, tiled=True)]
    reduce_sum x1 -> x0, other arithmetic: 3.42 us -> none  [local(): counts = jnp.sum(onehot.astype(jnp.float32), axis=1)]
    unnamed x1 -> x0, local copies, waits for them, and re-layouts: 1.62 us -> none
    transpose x2 -> x0, local copies, waits for them, and re-layouts: 1.37 us -> none  [local(): rows = rows.reshape(n_vocab, CAP, n_data, width).transpose(0, 2, 1, 3)]
  transfers between devices with their start and end apart: 2 -> 0, of which waited for: 2 -> 0; matrix products, arithmetic and copies ran while one was open for 14% -> 0% of each run, Pallas kernels for 0% -> 0%
where the time goes in v2:
time: 50.5 us; the launch traced here: 50.3 us
  blocking collectives  36.5 us (72%)
  Pallas kernels  13.1 us (26%)
  between operations  0.64 us (1%)
    all_to_all x1, blocking collectives, local(): got = lax.all_to_all(sent, AXES, split_axis=0, concat_axis=0, tiled=True)  36.5 us
    pallas_call x1, Pallas kernels, make_table(): pl.pallas_call(functools.partial(table_kernel, scale), out_shape=(jax.Sha...  10.4 us
    pallas_call x1, Pallas kernels, pack(): pl.pallas_call(functools.partial(pack_kernel, n_vocab, n_data), out_shape...  2.71 us

profile of v2, /device:TPU:0, one launch (start us, length us, event | category | flops | bytes accessed | tf_op | source)
XLA Modules:
  0.0 50.3 jit_solution(11936788742651307922)
XLA Ops:
  0.6 2.7 %pack.1 = bf16[32,136,128]{2,1,0:T(8,128)(2,1)} custom-call(bf16[128,4096]{1,0:T(8,128)(2,1)} %rows_hbm.1, s32[1,128]{1,0:T(1,128)} %bitcast.3), custom_call_target="tpu_custom_call" | custom-call | tf_op jit(solution)/shard_map/pack/pallas_call | solution.py:83
  3.3 36.5 %all_to_all.5.got = bf16[32,136,128]{2,1,0:T(8,128)(2,1)S(1)} all-to-all(bf16[32,136,128]{2,1,0:T(8,128)(2,1)} %pack.1), channel_id=1, replica_groups=mesh['vocab'=4,'dp'=8] {'vocab','dp'}, dimensions={0} | all-to-all | bytes 2228224 | tf_op jit(solution)/shard_map/all_to_all | solution.py:265
  39.9 10.4 %table.1 = (f32[8016,512]{1,0:T(8,128)}, f32[64,128]{1,0:T(8,128)}) custom-call(bf16[32,136,128]{2,1,0:T(8,128)(2,1)S(1)} %all_to_all.5.got), custom_call_target="tpu_custom_call" | custom-call | tf_op jit(solution)/shard_map/table/pallas_call | solution.py:234

commit v3 on v2

--- a/solution.py
+++ b/solution.py
@@ -15,8 +15,7 @@
 GROUP = LANES // CAP
 ID_ROWS = 8
 BLOCK = 512
-PAIR = 2
-BLOCKS = -(-VOCAB_DEV // (BLOCK * PAIR)) * PAIR
+BLOCKS = -(-VOCAB_DEV // BLOCK)
 WINDOW = 256
 
 
@@ -96,7 +95,7 @@
 
 
 def table_kernel(
-    scale, got, table_hbm, share_ref, x, ids_s, key_s, column_s, rank_s, sorted_ids, sorted_columns, sorted_x, table, starts, sem
+    scale, got, table_hbm, share_hbm, x, ids_s, key_s, column_s, rank_s, sorted_ids, sorted_columns, sorted_x, table, share, starts, sem
 ):
     sources, length, _ = got.shape
     total = sources * CAP
@@ -135,30 +134,27 @@
     for p in range(chunks):
         rank_s[p : p + 1, :] = jnp.sum(before[p], axis=0, keepdims=True)
 
+    sorted_ids[...] = jnp.full(sorted_ids.shape, -1, jnp.int32)
+    sorted_columns[...] = jnp.full(sorted_columns.shape, -1, jnp.int32)
+    sorted_x[...] = jnp.zeros(sorted_x.shape, x.dtype)
     flat = jnp.concatenate([ids[p : p + 1, :] for p in range(chunks)], axis=1)
     pick = lax.broadcasted_iota(jnp.int32, (8, total), 0)
     parts = jnp.where(pick == 0, lax.shift_right_arithmetic(flat, 7), jnp.bitwise_and(flat, 127))
     parts = parts.astype(jnp.float32).astype(x.dtype)
 
-    def order(c, _):
+    def order(c):
         place = lax.broadcasted_iota(jnp.int32, (WINDOW, LANES), 0) + c * WINDOW
         move = jnp.concatenate(
             [jnp.where(rank_s[p : p + 1, :] == place, 1.0, 0.0).astype(x.dtype) for p in range(chunks)], axis=1
         )
-        at = pl.ds(pl.multiple_of(c * WINDOW, WINDOW), WINDOW)
-        sorted_x[at, :] = jnp.dot(move, x[...], preferred_element_type=jnp.float32).astype(x.dtype)
+        sorted_x[c * WINDOW : (c + 1) * WINDOW, :] = jnp.dot(move, x[...], preferred_element_type=jnp.float32).astype(x.dtype)
         moved = lax.dot_general(parts, move, (((1,), (1,)), ((), ())), preferred_element_type=jnp.float32)
         moved = (moved[0:1] * 128.0 + moved[1:2]).astype(jnp.int32)
         for i in range(WINDOW // LANES):
-            sorted_ids[pl.ds(c * (WINDOW // LANES) + i, 1), :] = moved[:, i * LANES : (i + 1) * LANES]
-        return 0
-
-    lax.fori_loop(0, total // WINDOW, order, 0)
-    sorted_ids[chunks : chunks + 8, :] = jnp.full((8, LANES), -1, jnp.int32)
-    sorted_x[total : total + LANES, :] = jnp.zeros((LANES, x.shape[1]), x.dtype)
-    turned = sorted_ids[...].T
-    for q in range(chunks + 1):
-        sorted_columns[q * LANES : (q + 1) * LANES, :] = jnp.broadcast_to(turned[:, q : q + 1], (LANES, LANES))
+            at = c * (WINDOW // LANES) + i
+            sorted_ids[at : at + 1, :] = moved[:, i * LANES : (i + 1) * LANES]
+            turned = jnp.broadcast_to(moved[:, i * LANES : (i + 1) * LANES], (8, LANES)).T
+            sorted_columns[at * LANES : (at + 1) * LANES, :] = jnp.broadcast_to(turned[:, 0:1], (LANES, LANES))
 
     def rows_of(b, k):
         place = lax.broadcasted_iota(jnp.int32, (BLOCK, LANES), 0) + b * BLOCK
@@ -183,47 +179,62 @@
             axis=0,
         )
 
-    last = BLOCKS - 1
-    rest = VOCAB_DEV - last * BLOCK
-
-    def out_copy(b, n):
-        at = pl.ds(pl.multiple_of(b * BLOCK, BLOCK), n)
+    def out_copy(b):
+        at = pl.ds(b * BLOCK, min(BLOCK, VOCAB_DEV - b * BLOCK))
         return pltpu.make_async_copy(table.at[at, :], table_hbm.at[at, :], sem.at[b])
 
-    def build(step, _):
-        for i in range(PAIR):
-            b = step * PAIR + i
-            k = jnp.minimum(lax.shift_right_logical(starts[b], 7), chunks - 1)
-            table[pl.ds(pl.multiple_of(b * BLOCK, BLOCK), BLOCK), :] = rows_of(b, k)
-            share_ref[pl.ds(b * (BLOCK // LANES), BLOCK // LANES), :] = counts_of(b, k) * scale
-        for i in range(PAIR):
-            b = step * PAIR + i
-            k = jnp.minimum(lax.shift_right_logical(starts[b], 7), chunks - 1)
-            more = lax.div(jnp.maximum(starts[b + 1] - k * LANES - 1, 0), WINDOW)
-
-            def further(w, _, b=b, k=k):
-                at = pl.ds(pl.multiple_of(b * BLOCK, BLOCK), BLOCK)
-                table[at, :] += rows_of(b, k + w * (WINDOW // LANES))
-                at = pl.ds(b * (BLOCK // LANES), BLOCK // LANES)
-                share_ref[at, :] += counts_of(b, k + w * (WINDOW // LANES)) * scale
+    def window_of(b):
+        return jnp.minimum(lax.shift_right_logical(starts[b], 7), chunks - 1)
+
+    def build(b):
+        k = window_of(b)
+        table[b * BLOCK : (b + 1) * BLOCK, :] = rows_of(b, k)
+        share[b * (BLOCK // LANES) : (b + 1) * (BLOCK // LANES), :] = counts_of(b, k) * scale
+        out_copy(b).start()
+
+    windows = total // WINDOW
+    short = jnp.int32(0)
+    built = 0
+    for c in range(windows):
+        order(c)
+        ready = BLOCKS if c == windows - 1 else max((c + 1) * BLOCKS // windows - 2, 0)
+        for b in range(built, ready):
+            build(b)
+        if ready > built:
+            short = jnp.maximum(short, starts[ready] - (c + 1) * WINDOW)
+        built = max(built, ready)
+    for b in range(BLOCKS):
+        short = jnp.maximum(short, starts[b + 1] - window_of(b) * LANES - WINDOW)
+
+    @pl.when(short > 0)
+    def _():
+        for b in range(BLOCKS):
+            out_copy(b).wait()
+
+        def again(b, _):
+            at = pl.ds(pl.multiple_of(b * BLOCK, BLOCK), BLOCK)
+            share_at = pl.ds(b * (BLOCK // LANES), BLOCK // LANES)
+            table[at, :] = jnp.zeros((BLOCK, table.shape[1]), jnp.float32)
+            share[share_at, :] = jnp.zeros((BLOCK // LANES, LANES), jnp.float32)
+
+            def window(w, _):
+                k = window_of(b) + w * (WINDOW // LANES)
+                table[at, :] += rows_of(b, k)
+                share[share_at, :] += counts_of(b, k) * scale
                 return 0
 
-            lax.fori_loop(1, more + 1, further, 0)
-
-            @pl.when(b < last)
-            def _(b=b):
-                out_copy(b, BLOCK).start()
-
-            @pl.when(b == last)
-            def _():
-                out_copy(last, rest).start()
-
-        return 0
-
-    lax.fori_loop(0, BLOCKS // PAIR, build, 0)
-    for b in range(last):
-        out_copy(b, BLOCK).wait()
-    out_copy(last, rest).wait()
+            count = lax.div(jnp.maximum(starts[b + 1] - window_of(b) * LANES + WINDOW - 1, 0), WINDOW)
+            return lax.fori_loop(0, count, window, 0)
+
+        lax.fori_loop(0, BLOCKS, again, 0)
+        for b in range(BLOCKS):
+            out_copy(b).start()
+
+    share_copy = pltpu.make_async_copy(share, share_hbm, sem.at[BLOCKS])
+    share_copy.start()
+    for b in range(BLOCKS):
+        out_copy(b).wait()
+    share_copy.wait()
 
 
 def make_table(got, scale):
@@ -238,7 +249,7 @@
             jax.ShapeDtypeStruct((BLOCKS * BLOCK // LANES, LANES), jnp.float32),
         ),
         in_specs=[pl.BlockSpec(memory_space=pltpu.VMEM)],
-        out_specs=(pl.BlockSpec(memory_space=pl.ANY), pl.BlockSpec(memory_space=pltpu.VMEM)),
+        out_specs=(pl.BlockSpec(memory_space=pl.ANY), pl.BlockSpec(memory_space=pl.ANY)),
         scratch_shapes=[
             pltpu.VMEM((total, width), got.dtype),
             pltpu.VMEM((chunks, LANES), jnp.int32),
@@ -249,8 +260,9 @@
             pltpu.VMEM((total + LANES, LANES), jnp.int32),
             pltpu.VMEM((total + LANES, width), got.dtype),
             pltpu.VMEM((BLOCKS * BLOCK, width), jnp.float32),
+            pltpu.VMEM((BLOCKS * BLOCK // LANES, LANES), jnp.float32),
             pltpu.SMEM((BLOCKS + 1,), jnp.int32),
-            pltpu.SemaphoreType.DMA((BLOCKS,)),
+            pltpu.SemaphoreType.DMA((BLOCKS + 1,)),
         ],
         compiler_params=pltpu.CompilerParams(vmem_limit_bytes=48 * 1024 * 1024),
         name="table",

time: 50.5 us -> 48.4 us (0.958)
  Pallas kernels: 13.1 us -> 11 us
    pallas_call x1, Pallas kernels: 10.4 us -> 8.3 us  [make_table(): pl.pallas_call(functools.partial(table_kernel, scale), out_shape=(jax.Sha...]
where the time goes in v3:
time: 48.4 us; the launch traced here: 48.2 us
  blocking collectives  36.5 us (75%)
  Pallas kernels  11 us (23%)
  between operations  0.64 us (1%)
    all_to_all x1, blocking collectives, local(): got = lax.all_to_all(sent, AXES, split_axis=0, concat_axis=0, tiled=True)  36.5 us
    pallas_call x1, Pallas kernels, make_table(): pl.pallas_call(functools.partial(table_kernel, scale), out_shape=(jax.Sha...  8.3 us
    pallas_call x1, Pallas kernels, pack(): pl.pallas_call(functools.partial(pack_kernel, n_vocab, n_data), out_shape...  2.71 us

profile of v3, /device:TPU:0, one launch (start us, length us, event | category | flops | bytes accessed | tf_op | source)
XLA Modules:
  0.0 48.2 jit_solution(16349727987537047006)
XLA Ops:
  0.6 2.7 %pack.1 = bf16[32,136,128]{2,1,0:T(8,128)(2,1)} custom-call(bf16[128,4096]{1,0:T(8,128)(2,1)} %rows_hbm.1, s32[1,128]{1,0:T(1,128)} %bitcast.3), custom_call_target="tpu_custom_call" | custom-call | tf_op jit(solution)/shard_map/pack/pallas_call | solution.py:82
  3.3 36.5 %all_to_all.5.got = bf16[32,136,128]{2,1,0:T(8,128)(2,1)S(1)} all-to-all(bf16[32,136,128]{2,1,0:T(8,128)(2,1)} %pack.1), channel_id=1, replica_groups=mesh['vocab'=4,'dp'=8] {'vocab','dp'}, dimensions={0} | all-to-all | bytes 2228224 | tf_op jit(solution)/shard_map/all_to_all | solution.py:277
  39.9 8.3 %table.1 = (f32[8016,512]{1,0:T(8,128)}, f32[64,128]{1,0:T(8,128)}) custom-call(bf16[32,136,128]{2,1,0:T(8,128)(2,1)S(1)} %all_to_all.5.got), custom_call_target="tpu_custom_call" | custom-call | tf_op jit(solution)/shard_map/table/pallas_call | solution.py:245

commit v4 on v3

--- a/solution.py
+++ b/solution.py
@@ -94,9 +94,7 @@
     )(rows, ids)
 
 
-def table_kernel(
-    scale, got, table_hbm, share_hbm, x, ids_s, key_s, column_s, rank_s, sorted_ids, sorted_columns, sorted_x, table, share, starts, sem
-):
+def table_kernel(scale, got, table_hbm, share_hbm, x, ids_s, sorted_ids, sorted_x, table, share, starts, sem):
     sources, length, _ = got.shape
     total = sources * CAP
     chunks = total // LANES
@@ -110,57 +108,55 @@
         ids_s[g * half : (g + 1) * half, :] = (coded[:half] * 128.0 + coded[half:]).astype(jnp.int32)
     ids = ids_s[...]
     ids = jnp.where(ids < 0, BLOCKS * BLOCK, ids)
-    token = lax.broadcasted_iota(jnp.int32, (chunks, LANES), 0) * LANES + lax.broadcasted_iota(
-        jnp.int32, (chunks, LANES), 1
-    )
-    key = ids * total + token
-    key_s[...] = key
-    turned = key.T
-    for q in range(chunks):
-        column_s[q * LANES : (q + 1) * LANES, :] = jnp.broadcast_to(turned[:, q : q + 1], (LANES, LANES))
     for b in range(BLOCKS + 1):
         starts[b] = jnp.sum((ids < b * BLOCK).astype(jnp.int32))
     for j in range(tiles):
         x[:, j * LANES : (j + 1) * LANES] = got[:, j * CAP : (j + 1) * CAP, :].reshape(total, LANES)
-
-    def count(q, before):
-        column = column_s[pl.ds(pl.multiple_of(q * LANES, LANES), LANES), :].reshape(LANES // 8, 8, LANES)
-        return tuple(
-            before[p] + jnp.sum((column < key_s[p : p + 1, :].reshape(1, 1, LANES)).astype(jnp.int32), axis=0)
-            for p in range(chunks)
-        )
-
-    before = lax.fori_loop(0, chunks, count, tuple(jnp.zeros((8, LANES), jnp.int32) for _ in range(chunks)))
-    for p in range(chunks):
-        rank_s[p : p + 1, :] = jnp.sum(before[p], axis=0, keepdims=True)
-
     sorted_ids[...] = jnp.full(sorted_ids.shape, -1, jnp.int32)
-    sorted_columns[...] = jnp.full(sorted_columns.shape, -1, jnp.int32)
     sorted_x[...] = jnp.zeros(sorted_x.shape, x.dtype)
+
+    block = lax.div(ids, BLOCK)
+    inside = [jnp.where(block == b, 1.0, 0.0) for b in range(BLOCKS)]
+    mask = jnp.concatenate(inside, axis=0).astype(x.dtype)
+    above = lax.broadcasted_iota(jnp.int32, (LANES, 2 * LANES), 0) < lax.broadcasted_iota(
+        jnp.int32, (LANES, 2 * LANES), 1
+    )
+    ahead = jnp.dot(mask, jnp.where(above, 1.0, 0.0).astype(x.dtype), preferred_element_type=jnp.float32)
+    groups = BLOCKS * chunks
+    below = lax.broadcasted_iota(jnp.int32, (groups, groups), 0) > lax.broadcasted_iota(jnp.int32, (groups, groups), 1)
+    earlier = jnp.dot(
+        jnp.where(below, 1.0, 0.0).astype(x.dtype), ahead[:, LANES:].astype(x.dtype), preferred_element_type=jnp.float32
+    )
+    ahead = ahead[:, :LANES] + earlier
+    place = jnp.where(block < BLOCKS, 0.0, float(total))
+    for b in range(BLOCKS):
+        place = place + inside[b] * ahead[b * chunks : (b + 1) * chunks]
+    place = place.astype(jnp.int32)
+
     flat = jnp.concatenate([ids[p : p + 1, :] for p in range(chunks)], axis=1)
     pick = lax.broadcasted_iota(jnp.int32, (8, total), 0)
     parts = jnp.where(pick == 0, lax.shift_right_arithmetic(flat, 7), jnp.bitwise_and(flat, 127))
     parts = parts.astype(jnp.float32).astype(x.dtype)
 
     def order(c):
-        place = lax.broadcasted_iota(jnp.int32, (WINDOW, LANES), 0) + c * WINDOW
+        at = lax.broadcasted_iota(jnp.int32, (WINDOW, LANES), 0) + c * WINDOW
         move = jnp.concatenate(
-            [jnp.where(rank_s[p : p + 1, :] == place, 1.0, 0.0).astype(x.dtype) for p in range(chunks)], axis=1
+            [jnp.where(place[p : p + 1, :] == at, 1.0, 0.0).astype(x.dtype) for p in range(chunks)], axis=1
         )
-        sorted_x[c * WINDOW : (c + 1) * WINDOW, :] = jnp.dot(move, x[...], preferred_element_type=jnp.float32).astype(x.dtype)
         moved = lax.dot_general(parts, move, (((1,), (1,)), ((), ())), preferred_element_type=jnp.float32)
         moved = (moved[0:1] * 128.0 + moved[1:2]).astype(jnp.int32)
         for i in range(WINDOW // LANES):
-            at = c * (WINDOW // LANES) + i
-            sorted_ids[at : at + 1, :] = moved[:, i * LANES : (i + 1) * LANES]
-            turned = jnp.broadcast_to(moved[:, i * LANES : (i + 1) * LANES], (8, LANES)).T
-            sorted_columns[at * LANES : (at + 1) * LANES, :] = jnp.broadcast_to(turned[:, 0:1], (LANES, LANES))
+            row = c * (WINDOW // LANES) + i
+            sorted_ids[row : row + 1, :] = moved[:, i * LANES : (i + 1) * LANES]
+        sorted_x[c * WINDOW : (c + 1) * WINDOW, :] = jnp.dot(
+            move, x[...], preferred_element_type=jnp.float32
+        ).astype(x.dtype)
 
     def rows_of(b, k):
-        place = lax.broadcasted_iota(jnp.int32, (BLOCK, LANES), 0) + b * BLOCK
+        row = lax.broadcasted_iota(jnp.int32, (BLOCK, LANES), 0) + b * BLOCK
         hit = jnp.concatenate(
             [
-                jnp.where(sorted_ids[pl.ds(k + i, 1), :] == place, 1.0, 0.0).astype(x.dtype)
+                jnp.where(sorted_ids[pl.ds(k + i, 1), :] == row, 1.0, 0.0).astype(x.dtype)
                 for i in range(WINDOW // LANES)
             ],
             axis=1,
@@ -168,29 +164,12 @@
         at = pl.ds(pl.multiple_of(k * LANES, LANES), WINDOW)
         return jnp.dot(hit, sorted_x[at, :], preferred_element_type=jnp.float32)
 
-    def counts_of(b, k):
-        column = sorted_columns[pl.ds(pl.multiple_of(k * LANES, LANES), WINDOW), :].reshape(WINDOW // 8, 8, LANES)
-        place = lax.broadcasted_iota(jnp.int32, (1, 1, LANES), 2) + b * BLOCK
-        return jnp.concatenate(
-            [
-                jnp.sum(jnp.sum((column == place + i * LANES).astype(jnp.float32), axis=0), axis=0, keepdims=True)
-                for i in range(BLOCK // LANES)
-            ],
-            axis=0,
-        )
-
     def out_copy(b):
         at = pl.ds(b * BLOCK, min(BLOCK, VOCAB_DEV - b * BLOCK))
         return pltpu.make_async_copy(table.at[at, :], table_hbm.at[at, :], sem.at[b])
 
     def window_of(b):
         return jnp.minimum(lax.shift_right_logical(starts[b], 7), chunks - 1)
-
-    def build(b):
-        k = window_of(b)
-        table[b * BLOCK : (b + 1) * BLOCK, :] = rows_of(b, k)
-        share[b * (BLOCK // LANES) : (b + 1) * (BLOCK // LANES), :] = counts_of(b, k) * scale
-        out_copy(b).start()
 
     windows = total // WINDOW
     short = jnp.int32(0)
@@ -199,13 +178,29 @@
         order(c)
         ready = BLOCKS if c == windows - 1 else max((c + 1) * BLOCKS // windows - 2, 0)
         for b in range(built, ready):
-            build(b)
+            table[b * BLOCK : (b + 1) * BLOCK, :] = rows_of(b, window_of(b))
+            out_copy(b).start()
         if ready > built:
             short = jnp.maximum(short, starts[ready] - (c + 1) * WINDOW)
         built = max(built, ready)
     for b in range(BLOCKS):
         short = jnp.maximum(short, starts[b + 1] - window_of(b) * LANES - WINDOW)
 
+    def spread(size, value):
+        of = lax.broadcasted_iota(jnp.int32, (size, LANES), 0)
+        return jnp.concatenate(
+            [jnp.where(value[p : p + 1, :] == of, 1.0, 0.0).astype(x.dtype) for p in range(chunks)], axis=1
+        )
+
+    share[...] = scale * lax.dot_general(
+        spread(BLOCKS * BLOCK // LANES, lax.shift_right_arithmetic(ids, 7)),
+        spread(LANES, jnp.bitwise_and(ids, 127)),
+        (((1,), (1,)), ((), ())),
+        preferred_element_type=jnp.float32,
+    )
+    share_copy = pltpu.make_async_copy(share, share_hbm, sem.at[BLOCKS])
+    share_copy.start()
+
     @pl.when(short > 0)
     def _():
         for b in range(BLOCKS):
@@ -213,14 +208,10 @@
 
         def again(b, _):
             at = pl.ds(pl.multiple_of(b * BLOCK, BLOCK), BLOCK)
-            share_at = pl.ds(b * (BLOCK // LANES), BLOCK // LANES)
             table[at, :] = jnp.zeros((BLOCK, table.shape[1]), jnp.float32)
-            share[share_at, :] = jnp.zeros((BLOCK // LANES, LANES), jnp.float32)
 
             def window(w, _):
-                k = window_of(b) + w * (WINDOW // LANES)
-                table[at, :] += rows_of(b, k)
-                share[share_at, :] += counts_of(b, k) * scale
+                table[at, :] += rows_of(b, window_of(b) + w * (WINDOW // LANES))
                 return 0
 
             count = lax.div(jnp.maximum(starts[b + 1] - window_of(b) * LANES + WINDOW - 1, 0), WINDOW)
@@ -230,8 +221,6 @@
         for b in range(BLOCKS):
             out_copy(b).start()
 
-    share_copy = pltpu.make_async_copy(share, share_hbm, sem.at[BLOCKS])
-    share_copy.start()
     for b in range(BLOCKS):
         out_copy(b).wait()
     share_copy.wait()
@@ -253,11 +242,7 @@
         scratch_shapes=[
             pltpu.VMEM((total, width), got.dtype),
             pltpu.VMEM((chunks, LANES), jnp.int32),
-            pltpu.VMEM((chunks, LANES), jnp.int32),
-            pltpu.VMEM((total, LANES), jnp.int32),
-            pltpu.VMEM((chunks, LANES), jnp.int32),
             pltpu.VMEM((chunks + 8, LANES), jnp.int32),
-            pltpu.VMEM((total + LANES, LANES), jnp.int32),
             pltpu.VMEM((total + LANES, width), got.dtype),
             pltpu.VMEM((BLOCKS * BLOCK, width), jnp.float32),
             pltpu.VMEM((BLOCKS * BLOCK // LANES, LANES), jnp.float32),

time: 48.4 us -> 47.6 us (0.983)
  Pallas kernels: 11 us -> 10.2 us
    pallas_call x1, Pallas kernels: 8.3 us -> 7.45 us  [make_table(): pl.pallas_call(functools.partial(table_kernel, scale), out_shape=(jax.Sha...]
where the time goes in v4:
time: 47.6 us; the launch traced here: 47.3 us
  blocking collectives  36.5 us (77%)
  Pallas kernels  10.2 us (21%)
  between operations  0.64 us (1%)
    all_to_all x1, blocking collectives, local(): got = lax.all_to_all(sent, AXES, split_axis=0, concat_axis=0, tiled=True)  36.5 us
    pallas_call x1, Pallas kernels, make_table(): pl.pallas_call(functools.partial(table_kernel, scale), out_shape=(jax.Sha...  7.45 us
    pallas_call x1, Pallas kernels, pack(): pl.pallas_call(functools.partial(pack_kernel, n_vocab, n_data), out_shape...  2.71 us

profile of v4, /device:TPU:0, one launch (start us, length us, event | category | flops | bytes accessed | tf_op | source)
XLA Modules:
  0.0 47.3 jit_solution(5616132127823408128)
XLA Ops:
  0.6 2.7 %pack.1 = bf16[32,136,128]{2,1,0:T(8,128)(2,1)} custom-call(bf16[128,4096]{1,0:T(8,128)(2,1)} %rows_hbm.1, s32[1,128]{1,0:T(1,128)} %bitcast.3), custom_call_target="tpu_custom_call" | custom-call | tf_op jit(solution)/shard_map/pack/pallas_call | solution.py:82
  3.3 36.5 %all_to_all.5.got = bf16[32,136,128]{2,1,0:T(8,128)(2,1)S(1)} all-to-all(bf16[32,136,128]{2,1,0:T(8,128)(2,1)} %pack.1), channel_id=1, replica_groups=mesh['vocab'=4,'dp'=8] {'vocab','dp'}, dimensions={0} | all-to-all | bytes 2228224 | tf_op jit(solution)/shard_map/all_to_all | solution.py:262
  39.9 7.4 %table.1 = (f32[8016,512]{1,0:T(8,128)}, f32[64,128]{1,0:T(8,128)}) custom-call(bf16[32,136,128]{2,1,0:T(8,128)(2,1)S(1)} %all_to_all.5.got), custom_call_target="tpu_custom_call" | custom-call | tf_op jit(solution)/shard_map/table/pallas_call | solution.py:234

commit v5 on v4

--- a/solution.py
+++ b/solution.py
@@ -39,8 +39,10 @@
     return rows.reshape(n_vocab * CAP, data.shape[1]), slot_ids.reshape(1, n_vocab * CAP)
 
 
-def pack_kernel(n_vocab, n_data, rows_hbm, ids_ref, out_hbm, rows, out, in_sem, out_sem):
+def pack_kernel(n_vocab, n_data, rows_hbm, ids_hbm, out_hbm, rows, ids_ref, out, in_sem, out_sem):
     tiles = rows.shape[1] // (n_data * LANES)
+    ids_copy = pltpu.make_async_copy(ids_hbm, ids_ref, in_sem.at[n_vocab])
+    ids_copy.start()
     loads = []
     for v in range(n_vocab):
         strip = pl.ds(v * CAP, CAP)
@@ -52,6 +54,7 @@
     row = lax.rem(lax.div(source, GROUP), ID_ROWS // 2)
     here = lax.div(lane, CAP) == lax.rem(source, GROUP)
     stores = []
+    ids_copy.wait()
     for v in range(n_vocab):
         ids = ids_ref[:, v * CAP : (v + 1) * CAP]
         ids = jnp.where(ids < 0, -1, ids - v * VOCAB_DEV)
@@ -82,12 +85,13 @@
     return pl.pallas_call(
         functools.partial(pack_kernel, n_vocab, n_data),
         out_shape=jax.ShapeDtypeStruct(shape, rows.dtype),
-        in_specs=[pl.BlockSpec(memory_space=pl.ANY), pl.BlockSpec(memory_space=pltpu.VMEM)],
+        in_specs=[pl.BlockSpec(memory_space=pl.ANY)] * 2,
         out_specs=pl.BlockSpec(memory_space=pl.ANY),
         scratch_shapes=[
             pltpu.VMEM(rows.shape, rows.dtype),
+            pltpu.VMEM(ids.shape, ids.dtype),
             pltpu.VMEM(shape, rows.dtype),
-            pltpu.SemaphoreType.DMA((n_vocab,)),
+            pltpu.SemaphoreType.DMA((n_vocab + 1,)),
             pltpu.SemaphoreType.DMA((n_vocab,)),
         ],
         name="pack",

time: 47.6 us -> 46.9 us (0.985)
  Pallas kernels: 10.2 us -> 9.52 us
    pallas_call x1, Pallas kernels: 2.71 us -> 2.07 us  [pack(): pl.pallas_call(functools.partial(pack_kernel, n_vocab, n_data), out_shape...]
where the time goes in v5:
time: 46.9 us; the launch traced here: 46.7 us
  blocking collectives  36.5 us (78%)
  Pallas kernels  9.52 us (20%)
  between operations  0.64 us (1%)
    all_to_all x1, blocking collectives, local(): got = lax.all_to_all(sent, AXES, split_axis=0, concat_axis=0, tiled=True)  36.5 us
    pallas_call x1, Pallas kernels, make_table(): pl.pallas_call(functools.partial(table_kernel, scale), out_shape=(jax.Sha...  7.45 us
    pallas_call x1, Pallas kernels, pack(): pl.pallas_call(functools.partial(pack_kernel, n_vocab, n_data), out_shape...  2.07 us

profile of v5, /device:TPU:0, one launch (start us, length us, event | category | flops | bytes accessed | tf_op | source)
XLA Modules:
  0.0 46.7 jit_solution(6280169414253223196)
XLA Ops:
  0.6 2.1 %pack.1 = bf16[32,136,128]{2,1,0:T(8,128)(2,1)} custom-call(bf16[128,4096]{1,0:T(8,128)(2,1)} %rows_hbm.1, s32[1,128]{1,0:T(1,128)} %bitcast.3), custom_call_target="tpu_custom_call" | custom-call | tf_op jit(solution)/shard_map/pack/pallas_call | solution.py:85
  2.7 36.5 %all_to_all.5.got = bf16[32,136,128]{2,1,0:T(8,128)(2,1)S(1)} all-to-all(bf16[32,136,128]{2,1,0:T(8,128)(2,1)} %pack.1), channel_id=1, replica_groups=mesh['vocab'=4,'dp'=8] {'vocab','dp'}, dimensions={0} | all-to-all | bytes 2228224 | tf_op jit(solution)/shard_map/all_to_all | solution.py:266
  39.3 7.4 %table.1 = (f32[8016,512]{1,0:T(8,128)}, f32[64,128]{1,0:T(8,128)}) custom-call(bf16[32,136,128]{2,1,0:T(8,128)(2,1)S(1)} %all_to_all.5.got), custom_call_target="tpu_custom_call" | custom-call | tf_op jit(solution)/shard_map/table/pallas_call | solution.py:238

commit v6 on v4

--- a/solution.py
+++ b/solution.py
@@ -7,13 +7,13 @@
 from jax.experimental.pallas import tpu as pltpu
 from jax.sharding import PartitionSpec as P
 
+
 VOCAB_DEV = 8016
 TOK_DEV = 128
 CAP = 32
 AXES = ("vocab", "dp")
 LANES = 128
 GROUP = LANES // CAP
-ID_ROWS = 8
 BLOCK = 512
 BLOCKS = -(-VOCAB_DEV // BLOCK)
 WINDOW = 256
@@ -39,27 +39,15 @@
     return rows.reshape(n_vocab * CAP, data.shape[1]), slot_ids.reshape(1, n_vocab * CAP)
 
 
-def pack_kernel(n_vocab, n_data, rows_hbm, ids_ref, out_hbm, rows, out, in_sem, out_sem):
+def pack_kernel(n_vocab, n_data, rows_hbm, out_hbm, rows, out, in_sem, out_sem):
     tiles = rows.shape[1] // (n_data * LANES)
     loads = []
     for v in range(n_vocab):
         strip = pl.ds(v * CAP, CAP)
         loads.append(pltpu.make_async_copy(rows_hbm.at[strip], rows.at[strip], in_sem.at[v]))
         loads[-1].start()
-    source = lax.axis_index("vocab") * n_data + lax.axis_index("dp")
-    lane = lax.broadcasted_iota(jnp.int32, (ID_ROWS, LANES), 1)
-    sub = lax.broadcasted_iota(jnp.int32, (ID_ROWS, LANES), 0)
-    row = lax.rem(lax.div(source, GROUP), ID_ROWS // 2)
-    here = lax.div(lane, CAP) == lax.rem(source, GROUP)
     stores = []
     for v in range(n_vocab):
-        ids = ids_ref[:, v * CAP : (v + 1) * CAP]
-        ids = jnp.where(ids < 0, -1, ids - v * VOCAB_DEV)
-        ids = jnp.concatenate([ids] * GROUP, axis=1)
-        high = lax.shift_right_arithmetic(ids, 7).astype(jnp.float32)
-        low = jnp.bitwise_and(ids, 127).astype(jnp.float32)
-        coded = jnp.where(here & (sub == row), high, 0.0) + jnp.where(here & (sub == row + ID_ROWS // 2), low, 0.0)
-        coded = coded.astype(out.dtype)
         loads[v].wait()
         for d in range(n_data):
             for j in range(tiles):
@@ -67,7 +55,6 @@
                 out[v * n_data + d, j * CAP : (j + 1) * CAP, :] = rows[
                     v * CAP : (v + 1) * CAP, column : column + LANES
                 ]
-            out[v * n_data + d, tiles * CAP : tiles * CAP + ID_ROWS, :] = coded
         strip = pl.ds(v * n_data, n_data)
         stores.append(pltpu.make_async_copy(out.at[strip], out_hbm.at[strip], out_sem.at[v]))
         stores[-1].start()
@@ -75,14 +62,12 @@
         store.wait()
 
 
-def pack(rows, ids, n_vocab, n_data):
-    width = rows.shape[1] // n_data
-    length = width // LANES * CAP + ID_ROWS
-    shape = (n_vocab * n_data, length, LANES)
+def pack(rows, n_vocab, n_data):
+    shape = (n_vocab * n_data, rows.shape[1] // (n_data * LANES) * CAP, LANES)
     return pl.pallas_call(
         functools.partial(pack_kernel, n_vocab, n_data),
         out_shape=jax.ShapeDtypeStruct(shape, rows.dtype),
-        in_specs=[pl.BlockSpec(memory_space=pl.ANY), pl.BlockSpec(memory_space=pltpu.VMEM)],
+        in_specs=[pl.BlockSpec(memory_space=pl.ANY)],
         out_specs=pl.BlockSpec(memory_space=pl.ANY),
         scratch_shapes=[
             pltpu.VMEM(rows.shape, rows.dtype),
@@ -91,27 +76,49 @@
             pltpu.SemaphoreType.DMA((n_vocab,)),
         ],
         name="pack",
-    )(rows, ids)
-
-
-def table_kernel(scale, got, table_hbm, share_hbm, x, ids_s, sorted_ids, sorted_x, table, share, starts, sem):
+    )(rows)
+
+
+def exchange_ids(ids, n_vocab, n_data):
+    def from_device(x, apart):
+        return lax.ppermute(x, AXES, [(i, i ^ apart) for i in range(n_vocab * n_data)])
+
+    ids = jnp.concatenate([ids, from_device(ids, 1)])
+    ids = jnp.concatenate([ids] + [from_device(ids, v * n_data) for v in range(1, n_vocab)])
+    return [ids] + [from_device(ids, z) for z in range(2, n_data, 2)]
+
+
+def table_kernel(scale, n_vocab, n_data, got, *refs):
+    parts_in = refs[: n_data // 2]
+    table_hbm, share_hbm, x, ids_s, sorted_ids, sorted_x, table, share, starts, sem = refs[n_data // 2 :]
     sources, length, _ = got.shape
     total = sources * CAP
     chunks = total // LANES
-    tiles = (length - ID_ROWS) // CAP
-    half = ID_ROWS // 2
-    per = half * GROUP
-    for g in range(sources // per):
-        coded = got[g * per, tiles * CAP :, :].astype(jnp.float32)
-        for s in range(g * per + 1, (g + 1) * per):
-            coded = coded + got[s, tiles * CAP :, :].astype(jnp.float32)
-        ids_s[g * half : (g + 1) * half, :] = (coded[:half] * 128.0 + coded[half:]).astype(jnp.int32)
+    tiles = length // CAP
+    vocab, data = lax.axis_index("vocab"), lax.axis_index("dp")
+    near = 2 * n_vocab
+    lane = lax.broadcasted_iota(jnp.int32, (near, LANES), 1)
+    sub = lax.broadcasted_iota(jnp.int32, (near, LANES), 0)
+    here = lax.div(lane, CAP) == lax.rem(sub, GROUP)
+    for z in range(n_data // 2):
+        mine = parts_in[z][:, :CAP]
+        for v in range(1, n_vocab):
+            mine = jnp.where(vocab == v, parts_in[z][:, v * CAP : (v + 1) * CAP], mine)
+        mine = jnp.where(here, jnp.concatenate([mine] * GROUP, axis=1), 0)
+        for i in range(near // GROUP):
+            row = z * (near // GROUP) + i
+            ids_s[row : row + 1, :] = jnp.sum(mine[i * GROUP : (i + 1) * GROUP], axis=0, keepdims=True)
     ids = ids_s[...]
-    ids = jnp.where(ids < 0, BLOCKS * BLOCK, ids)
+    ids = jnp.where(ids < 0, BLOCKS * BLOCK, ids - vocab * VOCAB_DEV)
     for b in range(BLOCKS + 1):
         starts[b] = jnp.sum((ids < b * BLOCK).astype(jnp.int32))
-    for j in range(tiles):
-        x[:, j * LANES : (j + 1) * LANES] = got[:, j * CAP : (j + 1) * CAP, :].reshape(total, LANES)
+    for z in range(n_data // 2):
+        for v in range(n_vocab):
+            for c in range(2):
+                source = jnp.bitwise_xor(vocab, v) * n_data + jnp.bitwise_xor(data, 2 * z + c)
+                at = ((z * n_vocab + v) * 2 + c) * CAP
+                for j in range(tiles):
+                    x[at : at + CAP, j * LANES : (j + 1) * LANES] = got[source, j * CAP : (j + 1) * CAP, :]
     sorted_ids[...] = jnp.full(sorted_ids.shape, -1, jnp.int32)
     sorted_x[...] = jnp.zeros(sorted_x.shape, x.dtype)
 
@@ -226,18 +233,18 @@
     share_copy.wait()
 
 
-def make_table(got, scale):
+def make_table(got, ids, scale, n_vocab, n_data):
     sources, length, _ = got.shape
     total = sources * CAP
     chunks = total // LANES
-    width = (length - ID_ROWS) // CAP * LANES
+    width = length // CAP * LANES
     return pl.pallas_call(
-        functools.partial(table_kernel, scale),
+        functools.partial(table_kernel, scale, n_vocab, n_data),
         out_shape=(
             jax.ShapeDtypeStruct((VOCAB_DEV, width), jnp.float32),
             jax.ShapeDtypeStruct((BLOCKS * BLOCK // LANES, LANES), jnp.float32),
         ),
-        in_specs=[pl.BlockSpec(memory_space=pltpu.VMEM)],
+        in_specs=[pl.BlockSpec(memory_space=pltpu.VMEM)] * (1 + len(ids)),
         out_specs=(pl.BlockSpec(memory_space=pl.ANY), pl.BlockSpec(memory_space=pl.ANY)),
         scratch_shapes=[
             pltpu.VMEM((total, width), got.dtype),
@@ -251,16 +258,16 @@
         ],
         compiler_params=pltpu.CompilerParams(vmem_limit_bytes=48 * 1024 * 1024),
         name="table",
-    )(got)
+    )(got, *ids)
 
 
 def local(grads, token_ids):
     n_vocab = lax.axis_size("vocab")
     n_data = lax.axis_size("dp")
     rows, ids = bucket(token_ids, grads, n_vocab)
-    sent = pack(rows, ids, n_vocab, n_data)
-    got = lax.all_to_all(sent, AXES, split_axis=0, concat_axis=0, tiled=True)
-    table, share = make_table(got, VOCAB_DEV / (TOK_DEV * n_data))
+    got = lax.all_to_all(pack(rows, n_vocab, n_data), AXES, split_axis=0, concat_axis=0, tiled=True)
+    ids = exchange_ids(ids, n_vocab, n_data)
+    table, share = make_table(got, ids, VOCAB_DEV / (TOK_DEV * n_data), n_vocab, n_data)
     return table, share.reshape(-1)[:VOCAB_DEV]
 
 

time: 47.6 us -> 45.5 us (0.956)
  blocking collectives: 36.5 us -> 0 us
  waiting for transfers between devices: 0 us -> 17.7 us
  starting transfers between devices: 0 us -> 15.9 us
  local copies, waits for them, and re-layouts: 0 us -> 0.67 us
  other arithmetic: 0 us -> 0.66 us
  Pallas kernels: 10.2 us -> 9.68 us
    all_to_all x1 -> x0, blocking collectives: 36.5 us -> none  [local(): got = lax.all_to_all(sent, AXES, split_axis=0, concat_axis=0, tiled=True)]
    ppermute x0 -> x7, waiting for transfers between devices: none -> 16.6 us  [from_device(): lax.ppermute(x, AXES, [(i, i ^ apart) for i in range(n_vocab * n_data)])]
    ppermute x0 -> x7, starting transfers between devices: none -> 8.61 us  [from_device(): lax.ppermute(x, AXES, [(i, i ^ apart) for i in range(n_vocab * n_data)])]
    all_to_all x0 -> x1, starting transfers between devices: none -> 7.33 us  [local(): lax.all_to_all(pack(rows, n_vocab, n_data), AXES, split_axis=0, concat_ax...]
    all_to_all x0 -> x1, waiting for transfers between devices: none -> 1.09 us  [local(): lax.all_to_all(pack(rows, n_vocab, n_data), AXES, split_axis=0, concat_ax...]
    pallas_call x1, Pallas kernels: 2.71 us -> 2.03 us  [pack(): pl.pallas_call(functools.partial(pack_kernel, n_vocab, n_data), out_shape...]
    concatenate x0 -> x1, local copies, waits for them, and re-layouts: none -> 0.67 us  [exchange_ids(): jnp.concatenate([ids] + [from_device(ids, v * n_data) for v in range(1, n...]
    concatenate x0 -> x1, other arithmetic: none -> 0.66 us  [exchange_ids(): ids = jnp.concatenate([ids, from_device(ids, 1)])]
  transfers between devices with their start and end apart: 0 -> 8, of which waited for: 0 -> 7; matrix products, arithmetic and copies ran while one was open for 0% -> 3% of each run, Pallas kernels for 0% -> 0%
where the time goes in v6:
time: 45.5 us; the launch traced here: 45.3 us
  waiting for transfers between devices  17.7 us (39%)
  starting transfers between devices  15.9 us (35%)
  Pallas kernels  9.68 us (21%)
  local copies, waits for them, and re-layouts  0.67 us (1%)
  other arithmetic  0.66 us (1%)
  between operations  0.65 us (1%)
    ppermute x7, waiting for transfers between devices, from_device(): lax.ppermute(x, AXES, [(i, i ^ apart) for i in range(n_vocab * n_data)])  16.6 us
    ppermute x7, starting transfers between devices, from_device(): lax.ppermute(x, AXES, [(i, i ^ apart) for i in range(n_vocab * n_data)])  8.61 us
    pallas_call x1, Pallas kernels, make_table(): pl.pallas_call(functools.partial(table_kernel, scale, n_vocab, n_data), o...  7.65 us
    all_to_all x1, starting transfers between devices, local(): lax.all_to_all(pack(rows, n_vocab, n_data), AXES, split_axis=0, concat_ax...  7.33 us
    pallas_call x1, Pallas kernels, pack(): pl.pallas_call(functools.partial(pack_kernel, n_vocab, n_data), out_shape...  2.03 us
    all_to_all x1, waiting for transfers between devices, local(): lax.all_to_all(pack(rows, n_vocab, n_data), AXES, split_axis=0, concat_ax...  1.09 us
  transfers between devices with their start and end apart: 8, of which 7 were waited for; matrix products, arithmetic and copies ran while one was open for 3% of the time, Pallas kernels for 0%

profile of v6, /device:TPU:0, one launch (start us, length us, event | category | flops | bytes accessed | tf_op | source)
XLA Modules:
  0.0 45.3 jit_solution(17937009763281340276)
XLA Ops:
  0.6 2.0 %pack.1 = bf16[32,128,128]{2,1,0:T(8,128)(2,1)} custom-call(bf16[128,4096]{1,0:T(8,128)(2,1)} %rows_hbm.1), custom_call_target="tpu_custom_call" | custom-call | tf_op jit(solution)/shard_map/pack/pallas_call | solution.py:67
  2.7 7.3 %all-to-all-start = ((bf16[32,128,128]{2,1,0:T(8,128)(2,1)}), bf16[32,128,128]{2,1,0:T(8,128)(2,1)S(1)}, u32[]{:S(2)}, u32[]{:S(2)}) async-start(bf16[32,128,128]{2,1,0:T(8,128)(2,1)} %pack.1), calls=%async_computation | async-start | bytes 2097152 | tf_op jit(solution)/shard_map/all_to_all | solution.py:268
  10.0 0.3 collective-permute-start
  10.3 1.0 %collective-permute-done = s32[1,128]{1,0:T(1,128)S(1)} collective-permute-done((s32[1,128]{1,0:T(1,128)}, s32[1,128]{1,0:T(1,128)S(1)}, u32[]{:S(2)}, u32[]{:S(2)}) %collective-permute-start) | collective-permute-done | bytes 544 | tf_op jit(solution)/shard_map/ppermute | solution.py:84
  11.4 0.7 %pad_add_fusion = s32[2,128]{1,0:T(2,128)S(1)} fusion(s32[1,128]{1,0:T(1,128)S(1)} %collective-permute-done, s32[1,128]{1,0:T(1,128)} %bitcast.4), kind=kLoop, calls=%fused_computation | loop fusion | flops 256 | bytes 2048 | tf_op jit(solution)/shard_map/concatenate | solution.py:86
  12.0 2.7 %collective-permute-start.3 = (s32[2,128]{1,0:T(2,128)S(1)}, s32[2,128]{1,0:T(2,128)S(1)}, u32[]{:S(2)}, u32[]{:S(2)}) collective-permute-start(s32[2,128]{1,0:T(2,128)S(1)} %pad_add_fusion), channel_id=1, source_target_pairs={{0,24},{1,25},{2,26},{3,27},{4,28},{5,29},{6,30},{7,31},{8,16},{9,... | collective-permute-start | bytes 3080 | tf_op jit(solution)/shard_map/ppermute | solution.py:84
  14.7 0.6 %collective-permute-start.2 = (s32[2,128]{1,0:T(2,128)S(1)}, s32[2,128]{1,0:T(2,128)S(1)}, u32[]{:S(2)}, u32[]{:S(2)}) collective-permute-start(s32[2,128]{1,0:T(2,128)S(1)} %pad_add_fusion), channel_id=1, source_target_pairs={{0,16},{1,17},{2,18},{3,19},{4,20},{5,21},{6,22},{7,23},{8,24},{9,... | collective-permute-start | bytes 3080 | tf_op jit(solution)/shard_map/ppermute | solution.py:84
  15.3 0.3 collective-permute-start.1
  15.5 2.7 %collective-permute-done.3 = s32[2,128]{1,0:T(2,128)S(1)} collective-permute-done((s32[2,128]{1,0:T(2,128)S(1)}, s32[2,128]{1,0:T(2,128)S(1)}, u32[]{:S(2)}, u32[]{:S(2)}) %collective-permute-start.3) | collective-permute-done | bytes 1056 | tf_op jit(solution)/shard_map/ppermute | solution.py:84
  18.2 0.1 collective-permute-done.2
  18.3 0.6 %collective-permute-done.1 = s32[2,128]{1,0:T(2,128)S(1)} collective-permute-done((s32[2,128]{1,0:T(2,128)S(1)}, s32[2,128]{1,0:T(2,128)S(1)}, u32[]{:S(2)}, u32[]{:S(2)}) %collective-permute-start.1) | collective-permute-done | bytes 1056 | tf_op jit(solution)/shard_map/ppermute | solution.py:84
  18.9 0.7 %concatenate.8.refs_0_ = s32[8,128]{1,0:T(8,128)S(1)} concatenate(s32[1,128]{1,0:T(1,128)} %bitcast.5, s32[1,128]{1,0:T(1,128)S(1)} %collective-permute-done, s32[2,128]{1,0:T(2,128)S(1)} %collective-permute-done.1, s32[2,128]{1,0:T(2,128)S(1)} %collective-permute-done.2, s32[2,128]{1,0:T(2,128)S(1)} %collective-permute-done.3), dimensions={0} | concatenate | bytes 8192 | tf_op jit(solution)/shard_map/concatenate | solution.py:87
  19.6 4.2 %collective-permute-start.6 = (s32[8,128]{1,0:T(8,128)S(1)}, s32[8,128]{1,0:T(8,128)S(1)}, u32[]{:S(2)}, u32[]{:S(2)}) collective-permute-start(s32[8,128]{1,0:T(8,128)S(1)} %concatenate.8.refs_0_), channel_id=1, source_target_pairs={{0,6},{1,7},{2,4},{3,5},{4,2},{5,3},{6,0},{7,1},{8,14},{9,15},{10,... | collective-permute-start | bytes 12296 | tf_op jit(solution)/shard_map/ppermute | solution.py:84
  23.7 0.0 collective-permute-start.5
  23.7 0.6 %collective-permute-start.4 = (s32[8,128]{1,0:T(8,128)S(1)}, s32[8,128]{1,0:T(8,128)S(1)}, u32[]{:S(2)}, u32[]{:S(2)}) collective-permute-start(s32[8,128]{1,0:T(8,128)S(1)} %concatenate.8.refs_0_), channel_id=1, source_target_pairs={{0,2},{1,3},{2,0},{3,1},{4,6},{5,7},{6,4},{7,5},{8,10},{9,11},{10,... | collective-permute-start | bytes 12296 | tf_op jit(solution)/shard_map/ppermute | solution.py:84
  24.4 7.3 %collective-permute-done.6.refs_3_ = s32[8,128]{1,0:T(8,128)S(1)} collective-permute-done((s32[8,128]{1,0:T(8,128)S(1)}, s32[8,128]{1,0:T(8,128)S(1)}, u32[]{:S(2)}, u32[]{:S(2)}) %collective-permute-start.6) | collective-permute-done | bytes 4128 | tf_op jit(solution)/shard_map/ppermute | solution.py:84
  31.7 4.8 %collective-permute-done.5.refs_2_ = s32[8,128]{1,0:T(8,128)S(1)} collective-permute-done((s32[8,128]{1,0:T(8,128)S(1)}, s32[8,128]{1,0:T(8,128)S(1)}, u32[]{:S(2)}, u32[]{:S(2)}) %collective-permute-start.5) | collective-permute-done | bytes 4128 | tf_op jit(solution)/shard_map/ppermute | solution.py:84
  36.6 0.0 collective-permute-done.4.refs_1_
  36.6 1.1 %all-to-all-done.got = bf16[32,128,128]{2,1,0:T(8,128)(2,1)S(1)} async-done(((bf16[32,128,128]{2,1,0:T(8,128)(2,1)}), bf16[32,128,128]{2,1,0:T(8,128)(2,1)S(1)}, u32[]{:S(2)}, u32[]{:S(2)}) %all-to-all-start) | async-done | bytes 1048608 | tf_op jit(solution)/shard_map/all_to_all | solution.py:268
  37.6 7.7 %table.1 = (f32[8016,512]{1,0:T(8,128)}, f32[64,128]{1,0:T(8,128)}) custom-call(bf16[32,128,128]{2,1,0:T(8,128)(2,1)S(1)} %all-to-all-done.got, s32[8,128]{1,0:T(8,128)S(1)} %concatenate.8.refs_0_, s32[8,128]{1,0:T(8,128)S(1)} %collective-permute-done.4.refs_1_, s32[8,128]{1,0:T(8,128)S(1)} %collective-permute-done.5.refs_2_, ...), custom_call_target="tpu_custom_call" | custom-call | tf_op jit(solution)/shard_map/table/pallas_call | solution.py:241
Async XLA Ops:
  2.7 35.0 %all-to-all-start = ((bf16[32,128,128]{2,1,0:T(8,128)(2,1)}), bf16[32,128,128]{2,1,0:T(8,128)(2,1)S(1)}, u32[]{:S(2)}, u32[]{:S(2)}) async-start(bf16[32,128,128]{2,1,0:T(8,128)(2,1)} %pack.1), calls=%async_computation | async-start | bytes 2097152 | tf_op jit(solution)/shard_map/all_to_all | solution.py:268
  10.0 1.4 %collective-permute-start = (s32[1,128]{1,0:T(1,128)}, s32[1,128]{1,0:T(1,128)S(1)}, u32[]{:S(2)}, u32[]{:S(2)}) collective-permute-start(s32[1,128]{1,0:T(1,128)} %bitcast.3), channel_id=1, source_target_pairs={{0,1},{1,0},{2,3},{3,2},{4,5},{5,4},{6,7},{7,6},{8,9},{9,8},{10,11... | collective-permute-start | bytes 1544 | tf_op jit(solution)/shard_map/ppermute | solution.py:84
  12.0 6.1 %collective-permute-start.3 = (s32[2,128]{1,0:T(2,128)S(1)}, s32[2,128]{1,0:T(2,128)S(1)}, u32[]{:S(2)}, u32[]{:S(2)}) collective-permute-start(s32[2,128]{1,0:T(2,128)S(1)} %pad_add_fusion), channel_id=1, source_target_pairs={{0,24},{1,25},{2,26},{3,27},{4,28},{5,29},{6,30},{7,31},{8,16},{9,... | collective-permute-start | bytes 3080 | tf_op jit(solution)/shard_map/ppermute | solution.py:84
  14.7 3.6 %collective-permute-start.2 = (s32[2,128]{1,0:T(2,128)S(1)}, s32[2,128]{1,0:T(2,128)S(1)}, u32[]{:S(2)}, u32[]{:S(2)}) collective-permute-start(s32[2,128]{1,0:T(2,128)S(1)} %pad_add_fusion), channel_id=1, source_target_pairs={{0,16},{1,17},{2,18},{3,19},{4,20},{5,21},{6,22},{7,23},{8,24},{9,... | collective-permute-start | bytes 3080 | tf_op jit(solution)/shard_map/ppermute | solution.py:84
  15.3 3.6 %collective-permute-start.1 = (s32[2,128]{1,0:T(2,128)S(1)}, s32[2,128]{1,0:T(2,128)S(1)}, u32[]{:S(2)}, u32[]{:S(2)}) collective-permute-start(s32[2,128]{1,0:T(2,128)S(1)} %pad_add_fusion), channel_id=1, source_target_pairs={{0,8},{1,9},{2,10},{3,11},{4,12},{5,13},{6,14},{7,15},{8,0},{9,1},... | collective-permute-start | bytes 3080 | tf_op jit(solution)/shard_map/ppermute | solution.py:84
  19.6 12.2 %collective-permute-start.6 = (s32[8,128]{1,0:T(8,128)S(1)}, s32[8,128]{1,0:T(8,128)S(1)}, u32[]{:S(2)}, u32[]{:S(2)}) collective-permute-start(s32[8,128]{1,0:T(8,128)S(1)} %concatenate.8.refs_0_), channel_id=1, source_target_pairs={{0,6},{1,7},{2,4},{3,5},{4,2},{5,3},{6,0},{7,1},{8,14},{9,15},{10,... | collective-permute-start | bytes 12296 | tf_op jit(solution)/shard_map/ppermute | solution.py:84
  23.7 12.8 %collective-permute-start.5 = (s32[8,128]{1,0:T(8,128)S(1)}, s32[8,128]{1,0:T(8,128)S(1)}, u32[]{:S(2)}, u32[]{:S(2)}) collective-permute-start(s32[8,128]{1,0:T(8,128)S(1)} %concatenate.8.refs_0_), channel_id=1, source_target_pairs={{0,4},{1,5},{2,6},{3,7},{4,0},{5,1},{6,2},{7,3},{8,12},{9,13},{10,... | collective-permute-start | bytes 12296 | tf_op jit(solution)/shard_map/ppermute | solution.py:84
  23.7 12.8 %collective-permute-start.4 = (s32[8,128]{1,0:T(8,128)S(1)}, s32[8,128]{1,0:T(8,128)S(1)}, u32[]{:S(2)}, u32[]{:S(2)}) collective-permute-start(s32[8,128]{1,0:T(8,128)S(1)} %concatenate.8.refs_0_), channel_id=1, source_target_pairs={{0,2},{1,3},{2,0},{3,1},{4,6},{5,7},{6,4},{7,5},{8,10},{9,11},{10,... | collective-permute-start | bytes 12296 | tf_op jit(solution)/shard_map/ppermute | solution.py:84

commit v7 on v6

--- a/solution.py
+++ b/solution.py
@@ -88,14 +88,12 @@
     return [ids] + [from_device(ids, z) for z in range(2, n_data, 2)]
 
 
-def table_kernel(scale, n_vocab, n_data, got, *refs):
+def place_kernel(n_vocab, n_data, *refs):
     parts_in = refs[: n_data // 2]
-    table_hbm, share_hbm, x, ids_s, sorted_ids, sorted_x, table, share, starts, sem = refs[n_data // 2 :]
-    sources, length, _ = got.shape
-    total = sources * CAP
-    chunks = total // LANES
-    tiles = length // CAP
-    vocab, data = lax.axis_index("vocab"), lax.axis_index("dp")
+    out, ids_s = refs[n_data // 2 :]
+    chunks = ids_s.shape[0]
+    total = chunks * LANES
+    vocab = lax.axis_index("vocab")
     near = 2 * n_vocab
     lane = lax.broadcasted_iota(jnp.int32, (near, LANES), 1)
     sub = lax.broadcasted_iota(jnp.int32, (near, LANES), 0)
@@ -110,6 +108,50 @@
             ids_s[row : row + 1, :] = jnp.sum(mine[i * GROUP : (i + 1) * GROUP], axis=0, keepdims=True)
     ids = ids_s[...]
     ids = jnp.where(ids < 0, BLOCKS * BLOCK, ids - vocab * VOCAB_DEV)
+    out[:chunks, :] = ids
+
+    block = lax.div(ids, BLOCK)
+    inside = [jnp.where(block == b, 1.0, 0.0) for b in range(BLOCKS)]
+    mask = jnp.concatenate(inside, axis=0).astype(jnp.bfloat16)
+    above = lax.broadcasted_iota(jnp.int32, (LANES, 2 * LANES), 0) < lax.broadcasted_iota(
+        jnp.int32, (LANES, 2 * LANES), 1
+    )
+    ahead = jnp.dot(mask, jnp.where(above, 1.0, 0.0).astype(jnp.bfloat16), preferred_element_type=jnp.float32)
+    groups = BLOCKS * chunks
+    below = lax.broadcasted_iota(jnp.int32, (groups, groups), 0) > lax.broadcasted_iota(jnp.int32, (groups, groups), 1)
+    earlier = jnp.dot(
+        jnp.where(below, 1.0, 0.0).astype(jnp.bfloat16), ahead[:, LANES:].astype(jnp.bfloat16), preferred_element_type=jnp.float32
+    )
+    ahead = ahead[:, :LANES] + earlier
+    place = jnp.where(block < BLOCKS, 0.0, float(total))
+    for b in range(BLOCKS):
+        place = place + inside[b] * ahead[b * chunks : (b + 1) * chunks]
+    out[chunks:, :] = place.astype(jnp.int32)
+
+
+def place_tokens(ids, n_vocab, n_data):
+    shape = (n_vocab * n_data * CAP // LANES, LANES)
+    return pl.pallas_call(
+        functools.partial(place_kernel, n_vocab, n_data),
+        out_shape=jax.ShapeDtypeStruct((2 * shape[0], LANES), jnp.int32),
+        in_specs=[pl.BlockSpec(memory_space=pltpu.VMEM)] * len(ids),
+        out_specs=pl.BlockSpec(memory_space=pltpu.VMEM),
+        scratch_shapes=[pltpu.VMEM(shape, jnp.int32)],
+        compiler_params=pltpu.CompilerParams(vmem_limit_bytes=4 * 1024 * 1024),
+        name="place",
+    )(*ids)
+
+
+def table_kernel(
+    scale, n_vocab, n_data, got, placed, table_hbm, share_hbm, x, sorted_ids, sorted_x, table, share, starts, sem
+):
+    sources, length, _ = got.shape
+    total = sources * CAP
+    chunks = total // LANES
+    tiles = length // CAP
+    vocab, data = lax.axis_index("vocab"), lax.axis_index("dp")
+    ids = placed[:chunks, :]
+    place = placed[chunks:, :]
     for b in range(BLOCKS + 1):
         starts[b] = jnp.sum((ids < b * BLOCK).astype(jnp.int32))
     for z in range(n_data // 2):
@@ -121,24 +163,6 @@
                     x[at : at + CAP, j * LANES : (j + 1) * LANES] = got[source, j * CAP : (j + 1) * CAP, :]
     sorted_ids[...] = jnp.full(sorted_ids.shape, -1, jnp.int32)
     sorted_x[...] = jnp.zeros(sorted_x.shape, x.dtype)
-
-    block = lax.div(ids, BLOCK)
-    inside = [jnp.where(block == b, 1.0, 0.0) for b in range(BLOCKS)]
-    mask = jnp.concatenate(inside, axis=0).astype(x.dtype)
-    above = lax.broadcasted_iota(jnp.int32, (LANES, 2 * LANES), 0) < lax.broadcasted_iota(
-        jnp.int32, (LANES, 2 * LANES), 1
-    )
-    ahead = jnp.dot(mask, jnp.where(above, 1.0, 0.0).astype(x.dtype), preferred_element_type=jnp.float32)
-    groups = BLOCKS * chunks
-    below = lax.broadcasted_iota(jnp.int32, (groups, groups), 0) > lax.broadcasted_iota(jnp.int32, (groups, groups), 1)
-    earlier = jnp.dot(
-        jnp.where(below, 1.0, 0.0).astype(x.dtype), ahead[:, LANES:].astype(x.dtype), preferred_element_type=jnp.float32
-    )
-    ahead = ahead[:, :LANES] + earlier
-    place = jnp.where(block < BLOCKS, 0.0, float(total))
-    for b in range(BLOCKS):
-        place = place + inside[b] * ahead[b * chunks : (b + 1) * chunks]
-    place = place.astype(jnp.int32)
 
     flat = jnp.concatenate([ids[p : p + 1, :] for p in range(chunks)], axis=1)
     pick = lax.broadcasted_iota(jnp.int32, (8, total), 0)
@@ -233,7 +257,7 @@
     share_copy.wait()
 
 
-def make_table(got, ids, scale, n_vocab, n_data):
+def make_table(got, placed, scale, n_vocab, n_data):
     sources, length, _ = got.shape
     total = sources * CAP
     chunks = total // LANES
@@ -244,11 +268,10 @@
             jax.ShapeDtypeStruct((VOCAB_DEV, width), jnp.float32),
             jax.ShapeDtypeStruct((BLOCKS * BLOCK // LANES, LANES), jnp.float32),
         ),
-        in_specs=[pl.BlockSpec(memory_space=pltpu.VMEM)] * (1 + len(ids)),
+        in_specs=[pl.BlockSpec(memory_space=pltpu.VMEM)] * 2,
         out_specs=(pl.BlockSpec(memory_space=pl.ANY), pl.BlockSpec(memory_space=pl.ANY)),
         scratch_shapes=[
             pltpu.VMEM((total, width), got.dtype),
-            pltpu.VMEM((chunks, LANES), jnp.int32),
             pltpu.VMEM((chunks + 8, LANES), jnp.int32),
             pltpu.VMEM((total + LANES, width), got.dtype),
             pltpu.VMEM((BLOCKS * BLOCK, width), jnp.float32),
@@ -258,7 +281,7 @@
         ],
         compiler_params=pltpu.CompilerParams(vmem_limit_bytes=48 * 1024 * 1024),
         name="table",
-    )(got, *ids)
+    )(got, placed)
 
 
 def local(grads, token_ids):
@@ -266,8 +289,8 @@
     n_data = lax.axis_size("dp")
     rows, ids = bucket(token_ids, grads, n_vocab)
     got = lax.all_to_all(pack(rows, n_vocab, n_data), AXES, split_axis=0, concat_axis=0, tiled=True)
-    ids = exchange_ids(ids, n_vocab, n_data)
-    table, share = make_table(got, ids, VOCAB_DEV / (TOK_DEV * n_data), n_vocab, n_data)
+    placed = place_tokens(exchange_ids(ids, n_vocab, n_data), n_vocab, n_data)
+    table, share = make_table(got, placed, VOCAB_DEV / (TOK_DEV * n_data), n_vocab, n_data)
     return table, share.reshape(-1)[:VOCAB_DEV]
 
 

time: 45.5 us -> 45.1 us (level)
  waiting for transfers between devices: 17.7 us -> 17.1 us
    all_to_all x1, waiting for transfers between devices: 1.09 us -> 0.49 us  [local(): lax.all_to_all(pack(rows, n_vocab, n_data), AXES, split_axis=0, concat_ax...]
    pallas_call x0 -> x1, Pallas kernels: none -> 0.59 us  [place_tokens(): pl.pallas_call(functools.partial(place_kernel, n_vocab, n_data), out_shap...]
    pallas_call x1, Pallas kernels: 7.65 us -> 7.17 us  [make_table(): pl.pallas_call(functools.partial(table_kernel, scale, n_vocab, n_data), o...]
  transfers between devices with their start and end apart: 8 -> 8, of which waited for: 7 -> 7; matrix products, arithmetic and copies ran while one was open for 3% -> 3% of each run, Pallas kernels for 0% -> 1%
where the time goes in v7:
time: 45.1 us; the launch traced here: 44.8 us
  waiting for transfers between devices  17.1 us (38%)
  starting transfers between devices  15.9 us (35%)
  Pallas kernels  9.78 us (22%)
  local copies, waits for them, and re-layouts  0.67 us (1%)
  other arithmetic  0.66 us (1%)
  between operations  0.66 us (1%)
    ppermute x7, waiting for transfers between devices, from_device(): lax.ppermute(x, AXES, [(i, i ^ apart) for i in range(n_vocab * n_data)])  16.6 us
    ppermute x7, starting transfers between devices, from_device(): lax.ppermute(x, AXES, [(i, i ^ apart) for i in range(n_vocab * n_data)])  8.61 us
    all_to_all x1, starting transfers between devices, local(): lax.all_to_all(pack(rows, n_vocab, n_data), AXES, split_axis=0, concat_ax...  7.33 us
    pallas_call x1, Pallas kernels, make_table(): pl.pallas_call(functools.partial(table_kernel, scale, n_vocab, n_data), o...  7.17 us
    pallas_call x1, Pallas kernels, pack(): pl.pallas_call(functools.partial(pack_kernel, n_vocab, n_data), out_shape...  2.03 us
  transfers between devices with their start and end apart: 8, of which 7 were waited for; matrix products, arithmetic and copies ran while one was open for 3% of the time, Pallas kernels for 1%

profile of v7, /device:TPU:0, one launch (start us, length us, event | category | flops | bytes accessed | tf_op | source)
XLA Modules:
  0.0 44.8 jit_solution(7573902942147318698)
XLA Ops:
  0.6 2.0 %pack.1 = bf16[32,128,128]{2,1,0:T(8,128)(2,1)} custom-call(bf16[128,4096]{1,0:T(8,128)(2,1)} %rows_hbm.1), custom_call_target="tpu_custom_call" | custom-call | tf_op jit(solution)/shard_map/pack/pallas_call | solution.py:67
  2.7 7.3 %all-to-all-start = ((bf16[32,128,128]{2,1,0:T(8,128)(2,1)}), bf16[32,128,128]{2,1,0:T(8,128)(2,1)S(1)}, u32[]{:S(2)}, u32[]{:S(2)}) async-start(bf16[32,128,128]{2,1,0:T(8,128)(2,1)} %pack.1), calls=%async_computation | async-start | bytes 2097152 | tf_op jit(solution)/shard_map/all_to_all | solution.py:291
  10.0 0.3 collective-permute-start
  10.3 1.0 %collective-permute-done = s32[1,128]{1,0:T(1,128)S(1)} collective-permute-done((s32[1,128]{1,0:T(1,128)}, s32[1,128]{1,0:T(1,128)S(1)}, u32[]{:S(2)}, u32[]{:S(2)}) %collective-permute-start) | collective-permute-done | bytes 544 | tf_op jit(solution)/shard_map/ppermute | solution.py:84
  11.4 0.7 %pad_add_fusion = s32[2,128]{1,0:T(2,128)S(1)} fusion(s32[1,128]{1,0:T(1,128)S(1)} %collective-permute-done, s32[1,128]{1,0:T(1,128)} %bitcast.4), kind=kLoop, calls=%fused_computation | loop fusion | flops 256 | bytes 2048 | tf_op jit(solution)/shard_map/concatenate | solution.py:86
  12.0 2.7 %collective-permute-start.3 = (s32[2,128]{1,0:T(2,128)S(1)}, s32[2,128]{1,0:T(2,128)S(1)}, u32[]{:S(2)}, u32[]{:S(2)}) collective-permute-start(s32[2,128]{1,0:T(2,128)S(1)} %pad_add_fusion), channel_id=1, source_target_pairs={{0,24},{1,25},{2,26},{3,27},{4,28},{5,29},{6,30},{7,31},{8,16},{9,... | collective-permute-start | bytes 3080 | tf_op jit(solution)/shard_map/ppermute | solution.py:84
  14.7 0.6 %collective-permute-start.2 = (s32[2,128]{1,0:T(2,128)S(1)}, s32[2,128]{1,0:T(2,128)S(1)}, u32[]{:S(2)}, u32[]{:S(2)}) collective-permute-start(s32[2,128]{1,0:T(2,128)S(1)} %pad_add_fusion), channel_id=1, source_target_pairs={{0,16},{1,17},{2,18},{3,19},{4,20},{5,21},{6,22},{7,23},{8,24},{9,... | collective-permute-start | bytes 3080 | tf_op jit(solution)/shard_map/ppermute | solution.py:84
  15.3 0.3 collective-permute-start.1
  15.5 2.7 %collective-permute-done.3 = s32[2,128]{1,0:T(2,128)S(1)} collective-permute-done((s32[2,128]{1,0:T(2,128)S(1)}, s32[2,128]{1,0:T(2,128)S(1)}, u32[]{:S(2)}, u32[]{:S(2)}) %collective-permute-start.3) | collective-permute-done | bytes 1056 | tf_op jit(solution)/shard_map/ppermute | solution.py:84
  18.2 0.1 collective-permute-done.2
  18.3 0.6 %collective-permute-done.1 = s32[2,128]{1,0:T(2,128)S(1)} collective-permute-done((s32[2,128]{1,0:T(2,128)S(1)}, s32[2,128]{1,0:T(2,128)S(1)}, u32[]{:S(2)}, u32[]{:S(2)}) %collective-permute-start.1) | collective-permute-done | bytes 1056 | tf_op jit(solution)/shard_map/ppermute | solution.py:84
  18.9 0.7 %concatenate.8.refs_0_ = s32[8,128]{1,0:T(8,128)S(1)} concatenate(s32[1,128]{1,0:T(1,128)} %bitcast.5, s32[1,128]{1,0:T(1,128)S(1)} %collective-permute-done, s32[2,128]{1,0:T(2,128)S(1)} %collective-permute-done.1, s32[2,128]{1,0:T(2,128)S(1)} %collective-permute-done.2, s32[2,128]{1,0:T(2,128)S(1)} %collective-permute-done.3), dimensions={0} | concatenate | bytes 8192 | tf_op jit(solution)/shard_map/concatenate | solution.py:87
  19.6 4.2 %collective-permute-start.6 = (s32[8,128]{1,0:T(8,128)S(1)}, s32[8,128]{1,0:T(8,128)S(1)}, u32[]{:S(2)}, u32[]{:S(2)}) collective-permute-start(s32[8,128]{1,0:T(8,128)S(1)} %concatenate.8.refs_0_), channel_id=1, source_target_pairs={{0,6},{1,7},{2,4},{3,5},{4,2},{5,3},{6,0},{7,1},{8,14},{9,15},{10,... | collective-permute-start | bytes 12296 | tf_op jit(solution)/shard_map/ppermute | solution.py:84
  23.7 0.0 collective-permute-start.5
  23.7 0.6 %collective-permute-start.4 = (s32[8,128]{1,0:T(8,128)S(1)}, s32[8,128]{1,0:T(8,128)S(1)}, u32[]{:S(2)}, u32[]{:S(2)}) collective-permute-start(s32[8,128]{1,0:T(8,128)S(1)} %concatenate.8.refs_0_), channel_id=1, source_target_pairs={{0,2},{1,3},{2,0},{3,1},{4,6},{5,7},{6,4},{7,5},{8,10},{9,11},{10,... | collective-permute-start | bytes 12296 | tf_op jit(solution)/shard_map/ppermute | solution.py:84
  24.4 7.3 %collective-permute-done.6.refs_3_ = s32[8,128]{1,0:T(8,128)S(1)} collective-permute-done((s32[8,128]{1,0:T(8,128)S(1)}, s32[8,128]{1,0:T(8,128)S(1)}, u32[]{:S(2)}, u32[]{:S(2)}) %collective-permute-start.6) | collective-permute-done | bytes 4128 | tf_op jit(solution)/shard_map/ppermute | solution.py:84
  31.7 4.8 %collective-permute-done.5.refs_2_ = s32[8,128]{1,0:T(8,128)S(1)} collective-permute-done((s32[8,128]{1,0:T(8,128)S(1)}, s32[8,128]{1,0:T(8,128)S(1)}, u32[]{:S(2)}, u32[]{:S(2)}) %collective-permute-start.5) | collective-permute-done | bytes 4128 | tf_op jit(solution)/shard_map/ppermute | solution.py:84
  36.6 0.0 collective-permute-done.4.refs_1_
  36.6 0.6 %place.1.placed = s32[16,128]{1,0:T(8,128)S(1)} custom-call(s32[8,128]{1,0:T(8,128)S(1)} %concatenate.8.refs_0_, s32[8,128]{1,0:T(8,128)S(1)} %collective-permute-done.4.refs_1_, s32[8,128]{1,0:T(8,128)S(1)} %collective-permute-done.5.refs_2_, s32[8,128]{1,0:T(8,128)S(1)} %collective-permute-done.6.refs_3_), custom_call_target="tpu_custom_call" | custom-call | tf_op jit(solution)/shard_map/place/pallas_call | solution.py:134
  37.2 0.5 %all-to-all-done.got = bf16[32,128,128]{2,1,0:T(8,128)(2,1)S(1)} async-done(((bf16[32,128,128]{2,1,0:T(8,128)(2,1)}), bf16[32,128,128]{2,1,0:T(8,128)(2,1)S(1)}, u32[]{:S(2)}, u32[]{:S(2)}) %all-to-all-start) | async-done | bytes 1048608 | tf_op jit(solution)/shard_map/all_to_all | solution.py:291
  37.6 7.2 %table.1 = (f32[8016,512]{1,0:T(8,128)}, f32[64,128]{1,0:T(8,128)}) custom-call(bf16[32,128,128]{2,1,0:T(8,128)(2,1)S(1)} %all-to-all-done.got, s32[16,128]{1,0:T(8,128)S(1)} %place.1.placed), custom_call_target="tpu_custom_call" | custom-call | tf_op jit(solution)/shard_map/table/pallas_call | solution.py:265
Async XLA Ops:
  2.7 35.0 %all-to-all-start = ((bf16[32,128,128]{2,1,0:T(8,128)(2,1)}), bf16[32,128,128]{2,1,0:T(8,128)(2,1)S(1)}, u32[]{:S(2)}, u32[]{:S(2)}) async-start(bf16[32,128,128]{2,1,0:T(8,128)(2,1)} %pack.1), calls=%async_computation | async-start | bytes 2097152 | tf_op jit(solution)/shard_map/all_to_all | solution.py:291
  10.0 1.4 %collective-permute-start = (s32[1,128]{1,0:T(1,128)}, s32[1,128]{1,0:T(1,128)S(1)}, u32[]{:S(2)}, u32[]{:S(2)}) collective-permute-start(s32[1,128]{1,0:T(1,128)} %bitcast.3), channel_id=1, source_target_pairs={{0,1},{1,0},{2,3},{3,2},{4,5},{5,4},{6,7},{7,6},{8,9},{9,8},{10,11... | collective-permute-start | bytes 1544 | tf_op jit(solution)/shard_map/ppermute | solution.py:84
  12.0 6.1 %collective-permute-start.3 = (s32[2,128]{1,0:T(2,128)S(1)}, s32[2,128]{1,0:T(2,128)S(1)}, u32[]{:S(2)}, u32[]{:S(2)}) collective-permute-start(s32[2,128]{1,0:T(2,128)S(1)} %pad_add_fusion), channel_id=1, source_target_pairs={{0,24},{1,25},{2,26},{3,27},{4,28},{5,29},{6,30},{7,31},{8,16},{9,... | collective-permute-start | bytes 3080 | tf_op jit(solution)/shard_map/ppermute | solution.py:84
  14.7 3.6 %collective-permute-start.2 = (s32[2,128]{1,0:T(2,128)S(1)}, s32[2,128]{1,0:T(2,128)S(1)}, u32[]{:S(2)}, u32[]{:S(2)}) collective-permute-start(s32[2,128]{1,0:T(2,128)S(1)} %pad_add_fusion), channel_id=1, source_target_pairs={{0,16},{1,17},{2,18},{3,19},{4,20},{5,21},{6,22},{7,23},{8,24},{9,... | collective-permute-start | bytes 3080 | tf_op jit(solution)/shard_map/ppermute | solution.py:84
  15.3 3.6 %collective-permute-start.1 = (s32[2,128]{1,0:T(2,128)S(1)}, s32[2,128]{1,0:T(2,128)S(1)}, u32[]{:S(2)}, u32[]{:S(2)}) collective-permute-start(s32[2,128]{1,0:T(2,128)S(1)} %pad_add_fusion), channel_id=1, source_target_pairs={{0,8},{1,9},{2,10},{3,11},{4,12},{5,13},{6,14},{7,15},{8,0},{9,1},... | collective-permute-start | bytes 3080 | tf_op jit(solution)/shard_map/ppermute | solution.py:84
  19.6 12.2 %collective-permute-start.6 = (s32[8,128]{1,0:T(8,128)S(1)}, s32[8,128]{1,0:T(8,128)S(1)}, u32[]{:S(2)}, u32[]{:S(2)}) collective-permute-start(s32[8,128]{1,0:T(8,128)S(1)} %concatenate.8.refs_0_), channel_id=1, source_target_pairs={{0,6},{1,7},{2,4},{3,5},{4,2},{5,3},{6,0},{7,1},{8,14},{9,15},{10,... | collective-permute-start | bytes 12296 | tf_op jit(solution)/shard_map/ppermute | solution.py:84
  23.7 12.8 %collective-permute-start.5 = (s32[8,128]{1,0:T(8,128)S(1)}, s32[8,128]{1,0:T(8,128)S(1)}, u32[]{:S(2)}, u32[]{:S(2)}) collective-permute-start(s32[8,128]{1,0:T(8,128)S(1)} %concatenate.8.refs_0_), channel_id=1, source_target_pairs={{0,4},{1,5},{2,6},{3,7},{4,0},{5,1},{6,2},{7,3},{8,12},{9,13},{10,... | collective-permute-start | bytes 12296 | tf_op jit(solution)/shard_map/ppermute | solution.py:84
  23.7 12.8 %collective-permute-start.4 = (s32[8,128]{1,0:T(8,128)S(1)}, s32[8,128]{1,0:T(8,128)S(1)}, u32[]{:S(2)}, u32[]{:S(2)}) collective-permute-start(s32[8,128]{1,0:T(8,128)S(1)} %concatenate.8.refs_0_), channel_id=1, source_target_pairs={{0,2},{1,3},{2,0},{3,1},{4,6},{5,7},{6,4},{7,5},{8,10},{9,11},{10,... | collective-permute-start | bytes 12296 | tf_op jit(solution)/shard_map/ppermute | solution.py:84

commit v8 on v7

--- a/solution.py
+++ b/solution.py
@@ -88,9 +88,16 @@
     return [ids] + [from_device(ids, z) for z in range(2, n_data, 2)]
 
 
+def moves(place, c, dtype):
+    at = lax.broadcasted_iota(jnp.int32, (WINDOW, LANES), 0) + c * WINDOW
+    return jnp.concatenate(
+        [jnp.where(place[p : p + 1, :] == at, 1.0, 0.0).astype(dtype) for p in range(place.shape[0])], axis=1
+    )
+
+
 def place_kernel(n_vocab, n_data, *refs):
     parts_in = refs[: n_data // 2]
-    out, ids_s = refs[n_data // 2 :]
+    out, first, ids_s = refs[n_data // 2 :]
     chunks = ids_s.shape[0]
     total = chunks * LANES
     vocab = lax.axis_index("vocab")
@@ -126,16 +133,21 @@
     place = jnp.where(block < BLOCKS, 0.0, float(total))
     for b in range(BLOCKS):
         place = place + inside[b] * ahead[b * chunks : (b + 1) * chunks]
-    out[chunks:, :] = place.astype(jnp.int32)
+    place = place.astype(jnp.int32)
+    out[chunks:, :] = place
+    first[...] = moves(place, 0, first.dtype)
 
 
 def place_tokens(ids, n_vocab, n_data):
     shape = (n_vocab * n_data * CAP // LANES, LANES)
     return pl.pallas_call(
         functools.partial(place_kernel, n_vocab, n_data),
-        out_shape=jax.ShapeDtypeStruct((2 * shape[0], LANES), jnp.int32),
+        out_shape=(
+            jax.ShapeDtypeStruct((2 * shape[0], LANES), jnp.int32),
+            jax.ShapeDtypeStruct((WINDOW, shape[0] * LANES), jnp.bfloat16),
+        ),
         in_specs=[pl.BlockSpec(memory_space=pltpu.VMEM)] * len(ids),
-        out_specs=pl.BlockSpec(memory_space=pltpu.VMEM),
+        out_specs=(pl.BlockSpec(memory_space=pltpu.VMEM),) * 2,
         scratch_shapes=[pltpu.VMEM(shape, jnp.int32)],
         compiler_params=pltpu.CompilerParams(vmem_limit_bytes=4 * 1024 * 1024),
         name="place",
@@ -143,7 +155,7 @@
 
 
 def table_kernel(
-    scale, n_vocab, n_data, got, placed, table_hbm, share_hbm, x, sorted_ids, sorted_x, table, share, starts, sem
+    scale, n_vocab, n_data, got, placed, first, table_hbm, share_hbm, x, sorted_ids, sorted_x, table, share, starts, sem
 ):
     sources, length, _ = got.shape
     total = sources * CAP
@@ -170,10 +182,7 @@
     parts = parts.astype(jnp.float32).astype(x.dtype)
 
     def order(c):
-        at = lax.broadcasted_iota(jnp.int32, (WINDOW, LANES), 0) + c * WINDOW
-        move = jnp.concatenate(
-            [jnp.where(place[p : p + 1, :] == at, 1.0, 0.0).astype(x.dtype) for p in range(chunks)], axis=1
-        )
+        move = first[...] if c == 0 else moves(place, c, x.dtype)
         moved = lax.dot_general(parts, move, (((1,), (1,)), ((), ())), preferred_element_type=jnp.float32)
         moved = (moved[0:1] * 128.0 + moved[1:2]).astype(jnp.int32)
         for i in range(WINDOW // LANES):
@@ -257,7 +266,7 @@
     share_copy.wait()
 
 
-def make_table(got, placed, scale, n_vocab, n_data):
+def make_table(got, placed, first, scale, n_vocab, n_data):
     sources, length, _ = got.shape
     total = sources * CAP
     chunks = total // LANES
@@ -268,7 +277,7 @@
             jax.ShapeDtypeStruct((VOCAB_DEV, width), jnp.float32),
             jax.ShapeDtypeStruct((BLOCKS * BLOCK // LANES, LANES), jnp.float32),
         ),
-        in_specs=[pl.BlockSpec(memory_space=pltpu.VMEM)] * 2,
+        in_specs=[pl.BlockSpec(memory_space=pltpu.VMEM)] * 3,
         out_specs=(pl.BlockSpec(memory_space=pl.ANY), pl.BlockSpec(memory_space=pl.ANY)),
         scratch_shapes=[
             pltpu.VMEM((total, width), got.dtype),
@@ -281,7 +290,7 @@
         ],
         compiler_params=pltpu.CompilerParams(vmem_limit_bytes=48 * 1024 * 1024),
         name="table",
-    )(got, placed)
+    )(got, placed, first)
 
 
 def local(grads, token_ids):
@@ -289,8 +298,8 @@
     n_data = lax.axis_size("dp")
     rows, ids = bucket(token_ids, grads, n_vocab)
     got = lax.all_to_all(pack(rows, n_vocab, n_data), AXES, split_axis=0, concat_axis=0, tiled=True)
-    placed = place_tokens(exchange_ids(ids, n_vocab, n_data), n_vocab, n_data)
-    table, share = make_table(got, placed, VOCAB_DEV / (TOK_DEV * n_data), n_vocab, n_data)
+    placed, first = place_tokens(exchange_ids(ids, n_vocab, n_data), n_vocab, n_data)
+    table, share = make_table(got, placed, first, VOCAB_DEV / (TOK_DEV * n_data), n_vocab, n_data)
     return table, share.reshape(-1)[:VOCAB_DEV]
 
 

time: 45.1 us -> 45.1 us (level)
  transfers between devices with their start and end apart: 8 -> 8, of which waited for: 7 -> 7; matrix products, arithmetic and copies ran while one was open for 3% -> 3% of each run, Pallas kernels for 1% -> 2%
where the time goes in v8:
time: 45.1 us; the launch traced here: 44.8 us
  waiting for transfers between devices  16.9 us (37%)
  starting transfers between devices  15.9 us (35%)
  Pallas kernels  9.97 us (22%)
  local copies, waits for them, and re-layouts  0.67 us (1%)
  other arithmetic  0.66 us (1%)
  between operations  0.66 us (1%)
    ppermute x7, waiting for transfers between devices, from_device(): lax.ppermute(x, AXES, [(i, i ^ apart) for i in range(n_vocab * n_data)])  16.6 us
    ppermute x7, starting transfers between devices, from_device(): lax.ppermute(x, AXES, [(i, i ^ apart) for i in range(n_vocab * n_data)])  8.61 us
    all_to_all x1, starting transfers between devices, local(): lax.all_to_all(pack(rows, n_vocab, n_data), AXES, split_axis=0, concat_ax...  7.33 us
    pallas_call x1, Pallas kernels, make_table(): pl.pallas_call(functools.partial(table_kernel, scale, n_vocab, n_data), o...  7.17 us
    pallas_call x1, Pallas kernels, pack(): pl.pallas_call(functools.partial(pack_kernel, n_vocab, n_data), out_shape...  2.03 us
  transfers between devices with their start and end apart: 8, of which 7 were waited for; matrix products, arithmetic and copies ran while one was open for 3% of the time, Pallas kernels for 2%

profile of v8, /device:TPU:0, one launch (start us, length us, event | category | flops | bytes accessed | tf_op | source)
XLA Modules:
  0.0 44.8 jit_solution(4937918844542624225)
XLA Ops:
  0.6 2.0 %pack.1 = bf16[32,128,128]{2,1,0:T(8,128)(2,1)} custom-call(bf16[128,4096]{1,0:T(8,128)(2,1)} %rows_hbm.1), custom_call_target="tpu_custom_call" | custom-call | tf_op jit(solution)/shard_map/pack/pallas_call | solution.py:67
  2.7 7.3 %all-to-all-start = ((bf16[32,128,128]{2,1,0:T(8,128)(2,1)}), bf16[32,128,128]{2,1,0:T(8,128)(2,1)S(1)}, u32[]{:S(2)}, u32[]{:S(2)}) async-start(bf16[32,128,128]{2,1,0:T(8,128)(2,1)} %pack.1), calls=%async_computation | async-start | bytes 2097152 | tf_op jit(solution)/shard_map/all_to_all | solution.py:300
  10.0 0.3 collective-permute-start
  10.3 1.0 %collective-permute-done = s32[1,128]{1,0:T(1,128)S(1)} collective-permute-done((s32[1,128]{1,0:T(1,128)}, s32[1,128]{1,0:T(1,128)S(1)}, u32[]{:S(2)}, u32[]{:S(2)}) %collective-permute-start) | collective-permute-done | bytes 544 | tf_op jit(solution)/shard_map/ppermute | solution.py:84
  11.4 0.7 %pad_add_fusion = s32[2,128]{1,0:T(2,128)S(1)} fusion(s32[1,128]{1,0:T(1,128)S(1)} %collective-permute-done, s32[1,128]{1,0:T(1,128)} %bitcast.4), kind=kLoop, calls=%fused_computation | loop fusion | flops 256 | bytes 2048 | tf_op jit(solution)/shard_map/concatenate | solution.py:86
  12.0 2.7 %collective-permute-start.3 = (s32[2,128]{1,0:T(2,128)S(1)}, s32[2,128]{1,0:T(2,128)S(1)}, u32[]{:S(2)}, u32[]{:S(2)}) collective-permute-start(s32[2,128]{1,0:T(2,128)S(1)} %pad_add_fusion), channel_id=1, source_target_pairs={{0,24},{1,25},{2,26},{3,27},{4,28},{5,29},{6,30},{7,31},{8,16},{9,... | collective-permute-start | bytes 3080 | tf_op jit(solution)/shard_map/ppermute | solution.py:84
  14.7 0.6 %collective-permute-start.2 = (s32[2,128]{1,0:T(2,128)S(1)}, s32[2,128]{1,0:T(2,128)S(1)}, u32[]{:S(2)}, u32[]{:S(2)}) collective-permute-start(s32[2,128]{1,0:T(2,128)S(1)} %pad_add_fusion), channel_id=1, source_target_pairs={{0,16},{1,17},{2,18},{3,19},{4,20},{5,21},{6,22},{7,23},{8,24},{9,... | collective-permute-start | bytes 3080 | tf_op jit(solution)/shard_map/ppermute | solution.py:84
  15.3 0.3 collective-permute-start.1
  15.5 2.7 %collective-permute-done.3 = s32[2,128]{1,0:T(2,128)S(1)} collective-permute-done((s32[2,128]{1,0:T(2,128)S(1)}, s32[2,128]{1,0:T(2,128)S(1)}, u32[]{:S(2)}, u32[]{:S(2)}) %collective-permute-start.3) | collective-permute-done | bytes 1056 | tf_op jit(solution)/shard_map/ppermute | solution.py:84
  18.2 0.1 collective-permute-done.2
  18.3 0.6 %collective-permute-done.1 = s32[2,128]{1,0:T(2,128)S(1)} collective-permute-done((s32[2,128]{1,0:T(2,128)S(1)}, s32[2,128]{1,0:T(2,128)S(1)}, u32[]{:S(2)}, u32[]{:S(2)}) %collective-permute-start.1) | collective-permute-done | bytes 1056 | tf_op jit(solution)/shard_map/ppermute | solution.py:84
  18.9 0.7 %concatenate.8.refs_0_ = s32[8,128]{1,0:T(8,128)S(1)} concatenate(s32[1,128]{1,0:T(1,128)} %bitcast.5, s32[1,128]{1,0:T(1,128)S(1)} %collective-permute-done, s32[2,128]{1,0:T(2,128)S(1)} %collective-permute-done.1, s32[2,128]{1,0:T(2,128)S(1)} %collective-permute-done.2, s32[2,128]{1,0:T(2,128)S(1)} %collective-permute-done.3), dimensions={0} | concatenate | bytes 8192 | tf_op jit(solution)/shard_map/concatenate | solution.py:87
  19.6 4.2 %collective-permute-start.6 = (s32[8,128]{1,0:T(8,128)S(1)}, s32[8,128]{1,0:T(8,128)S(1)}, u32[]{:S(2)}, u32[]{:S(2)}) collective-permute-start(s32[8,128]{1,0:T(8,128)S(1)} %concatenate.8.refs_0_), channel_id=1, source_target_pairs={{0,6},{1,7},{2,4},{3,5},{4,2},{5,3},{6,0},{7,1},{8,14},{9,15},{10,... | collective-permute-start | bytes 12296 | tf_op jit(solution)/shard_map/ppermute | solution.py:84
  23.7 0.0 collective-permute-start.5
  23.7 0.6 %collective-permute-start.4 = (s32[8,128]{1,0:T(8,128)S(1)}, s32[8,128]{1,0:T(8,128)S(1)}, u32[]{:S(2)}, u32[]{:S(2)}) collective-permute-start(s32[8,128]{1,0:T(8,128)S(1)} %concatenate.8.refs_0_), channel_id=1, source_target_pairs={{0,2},{1,3},{2,0},{3,1},{4,6},{5,7},{6,4},{7,5},{8,10},{9,11},{10,... | collective-permute-start | bytes 12296 | tf_op jit(solution)/shard_map/ppermute | solution.py:84
  24.4 7.3 %collective-permute-done.6.refs_3_ = s32[8,128]{1,0:T(8,128)S(1)} collective-permute-done((s32[8,128]{1,0:T(8,128)S(1)}, s32[8,128]{1,0:T(8,128)S(1)}, u32[]{:S(2)}, u32[]{:S(2)}) %collective-permute-start.6) | collective-permute-done | bytes 4128 | tf_op jit(solution)/shard_map/ppermute | solution.py:84
  31.7 4.8 %collective-permute-done.5.refs_2_ = s32[8,128]{1,0:T(8,128)S(1)} collective-permute-done((s32[8,128]{1,0:T(8,128)S(1)}, s32[8,128]{1,0:T(8,128)S(1)}, u32[]{:S(2)}, u32[]{:S(2)}) %collective-permute-start.5) | collective-permute-done | bytes 4128 | tf_op jit(solution)/shard_map/ppermute | solution.py:84
  36.6 0.0 collective-permute-done.4.refs_1_
  36.6 0.8 %place.1 = (s32[16,128]{1,0:T(8,128)S(1)}, bf16[256,1024]{1,0:T(8,128)(2,1)S(1)}) custom-call(s32[8,128]{1,0:T(8,128)S(1)} %concatenate.8.refs_0_, s32[8,128]{1,0:T(8,128)S(1)} %collective-permute-done.4.refs_1_, s32[8,128]{1,0:T(8,128)S(1)} %collective-permute-done.5.refs_2_, s32[8,128]{1,0:T(8,128)S(1)} %collective-permute-done.6.refs_3_), custom_call_target="tpu_custom_call" | custom-call | tf_op jit(solution)/shard_map/place/pallas_call | solution.py:143
  37.3 0.3 all-to-all-done.got
  37.6 7.2 %table.1 = (f32[8016,512]{1,0:T(8,128)}, f32[64,128]{1,0:T(8,128)}) custom-call(bf16[32,128,128]{2,1,0:T(8,128)(2,1)S(1)} %all-to-all-done.got, s32[16,128]{1,0:T(8,128)S(1)} %get-tuple-element.6.placed, bf16[256,1024]{1,0:T(8,128)(2,1)S(1)} %get-tuple-element.7.first), custom_call_target="tpu_custom_call" | custom-call | tf_op jit(solution)/shard_map/table/pallas_call | solution.py:274
Async XLA Ops:
  2.7 35.0 %all-to-all-start = ((bf16[32,128,128]{2,1,0:T(8,128)(2,1)}), bf16[32,128,128]{2,1,0:T(8,128)(2,1)S(1)}, u32[]{:S(2)}, u32[]{:S(2)}) async-start(bf16[32,128,128]{2,1,0:T(8,128)(2,1)} %pack.1), calls=%async_computation | async-start | bytes 2097152 | tf_op jit(solution)/shard_map/all_to_all | solution.py:300
  10.0 1.4 %collective-permute-start = (s32[1,128]{1,0:T(1,128)}, s32[1,128]{1,0:T(1,128)S(1)}, u32[]{:S(2)}, u32[]{:S(2)}) collective-permute-start(s32[1,128]{1,0:T(1,128)} %bitcast.3), channel_id=1, source_target_pairs={{0,1},{1,0},{2,3},{3,2},{4,5},{5,4},{6,7},{7,6},{8,9},{9,8},{10,11... | collective-permute-start | bytes 1544 | tf_op jit(solution)/shard_map/ppermute | solution.py:84
  12.0 6.1 %collective-permute-start.3 = (s32[2,128]{1,0:T(2,128)S(1)}, s32[2,128]{1,0:T(2,128)S(1)}, u32[]{:S(2)}, u32[]{:S(2)}) collective-permute-start(s32[2,128]{1,0:T(2,128)S(1)} %pad_add_fusion), channel_id=1, source_target_pairs={{0,24},{1,25},{2,26},{3,27},{4,28},{5,29},{6,30},{7,31},{8,16},{9,... | collective-permute-start | bytes 3080 | tf_op jit(solution)/shard_map/ppermute | solution.py:84
  14.7 3.6 %collective-permute-start.2 = (s32[2,128]{1,0:T(2,128)S(1)}, s32[2,128]{1,0:T(2,128)S(1)}, u32[]{:S(2)}, u32[]{:S(2)}) collective-permute-start(s32[2,128]{1,0:T(2,128)S(1)} %pad_add_fusion), channel_id=1, source_target_pairs={{0,16},{1,17},{2,18},{3,19},{4,20},{5,21},{6,22},{7,23},{8,24},{9,... | collective-permute-start | bytes 3080 | tf_op jit(solution)/shard_map/ppermute | solution.py:84
  15.3 3.6 %collective-permute-start.1 = (s32[2,128]{1,0:T(2,128)S(1)}, s32[2,128]{1,0:T(2,128)S(1)}, u32[]{:S(2)}, u32[]{:S(2)}) collective-permute-start(s32[2,128]{1,0:T(2,128)S(1)} %pad_add_fusion), channel_id=1, source_target_pairs={{0,8},{1,9},{2,10},{3,11},{4,12},{5,13},{6,14},{7,15},{8,0},{9,1},... | collective-permute-start | bytes 3080 | tf_op jit(solution)/shard_map/ppermute | solution.py:84
  19.6 12.2 %collective-permute-start.6 = (s32[8,128]{1,0:T(8,128)S(1)}, s32[8,128]{1,0:T(8,128)S(1)}, u32[]{:S(2)}, u32[]{:S(2)}) collective-permute-start(s32[8,128]{1,0:T(8,128)S(1)} %concatenate.8.refs_0_), channel_id=1, source_target_pairs={{0,6},{1,7},{2,4},{3,5},{4,2},{5,3},{6,0},{7,1},{8,14},{9,15},{10,... | collective-permute-start | bytes 12296 | tf_op jit(solution)/shard_map/ppermute | solution.py:84
  23.7 12.8 %collective-permute-start.5 = (s32[8,128]{1,0:T(8,128)S(1)}, s32[8,128]{1,0:T(8,128)S(1)}, u32[]{:S(2)}, u32[]{:S(2)}) collective-permute-start(s32[8,128]{1,0:T(8,128)S(1)} %concatenate.8.refs_0_), channel_id=1, source_target_pairs={{0,4},{1,5},{2,6},{3,7},{4,0},{5,1},{6,2},{7,3},{8,12},{9,13},{10,... | collective-permute-start | bytes 12296 | tf_op jit(solution)/shard_map/ppermute | solution.py:84
  23.7 12.8 %collective-permute-start.4 = (s32[8,128]{1,0:T(8,128)S(1)}, s32[8,128]{1,0:T(8,128)S(1)}, u32[]{:S(2)}, u32[]{:S(2)}) collective-permute-start(s32[8,128]{1,0:T(8,128)S(1)} %concatenate.8.refs_0_), channel_id=1, source_target_pairs={{0,2},{1,3},{2,0},{3,1},{4,6},{5,7},{6,4},{7,5},{8,10},{9,11},{10,... | collective-permute-start | bytes 12296 | tf_op jit(solution)/shard_map/ppermute | solution.py:84

commit v9 on v7

--- a/solution.py
+++ b/solution.py
@@ -169,17 +169,17 @@
     parts = jnp.where(pick == 0, lax.shift_right_arithmetic(flat, 7), jnp.bitwise_and(flat, 127))
     parts = parts.astype(jnp.float32).astype(x.dtype)
 
-    def order(c):
-        at = lax.broadcasted_iota(jnp.int32, (WINDOW, LANES), 0) + c * WINDOW
+    def order(start, size):
+        at = lax.broadcasted_iota(jnp.int32, (size, LANES), 0) + start
         move = jnp.concatenate(
             [jnp.where(place[p : p + 1, :] == at, 1.0, 0.0).astype(x.dtype) for p in range(chunks)], axis=1
         )
         moved = lax.dot_general(parts, move, (((1,), (1,)), ((), ())), preferred_element_type=jnp.float32)
         moved = (moved[0:1] * 128.0 + moved[1:2]).astype(jnp.int32)
-        for i in range(WINDOW // LANES):
-            row = c * (WINDOW // LANES) + i
+        for i in range(size // LANES):
+            row = start // LANES + i
             sorted_ids[row : row + 1, :] = moved[:, i * LANES : (i + 1) * LANES]
-        sorted_x[c * WINDOW : (c + 1) * WINDOW, :] = jnp.dot(
+        sorted_x[start : start + size, :] = jnp.dot(
             move, x[...], preferred_element_type=jnp.float32
         ).astype(x.dtype)
 
@@ -192,7 +192,7 @@
             ],
             axis=1,
         )
-        at = pl.ds(pl.multiple_of(k * LANES, LANES), WINDOW)
+        at = pl.ds(k * LANES if isinstance(k, int) else pl.multiple_of(k * LANES, LANES), WINDOW)
         return jnp.dot(hit, sorted_x[at, :], preferred_element_type=jnp.float32)
 
     def out_copy(b):
@@ -200,19 +200,22 @@
         return pltpu.make_async_copy(table.at[at, :], table_hbm.at[at, :], sem.at[b])
 
     def window_of(b):
+        if isinstance(b, int) and b == 0:
+            return 0
         return jnp.minimum(lax.shift_right_logical(starts[b], 7), chunks - 1)
 
-    windows = total // WINDOW
     short = jnp.int32(0)
-    built = 0
-    for c in range(windows):
-        order(c)
-        ready = BLOCKS if c == windows - 1 else max((c + 1) * BLOCKS // windows - 2, 0)
+    built = done = 0
+    while done < total:
+        size = LANES
+        order(done, size)
+        done += size
+        ready = BLOCKS if done == total else max(done * BLOCKS // total - min(done // LANES, 2), 0)
         for b in range(built, ready):
             table[b * BLOCK : (b + 1) * BLOCK, :] = rows_of(b, window_of(b))
             out_copy(b).start()
         if ready > built:
-            short = jnp.maximum(short, starts[ready] - (c + 1) * WINDOW)
+            short = jnp.maximum(short, starts[ready] - done)
         built = max(built, ready)
     for b in range(BLOCKS):
         short = jnp.maximum(short, starts[b + 1] - window_of(b) * LANES - WINDOW)

time: 45.1 us -> 44.9 us (level)
  no operation moved by 1% of the time
where the time goes in v9:
time: 44.9 us; the launch traced here: 44.7 us
  waiting for transfers between devices  17.1 us (38%)
  starting transfers between devices  15.9 us (35%)
  Pallas kernels  9.63 us (21%)
  local copies, waits for them, and re-layouts  0.67 us (1%)
  other arithmetic  0.66 us (1%)
  between operations  0.66 us (1%)
    ppermute x7, waiting for transfers between devices, from_device(): lax.ppermute(x, AXES, [(i, i ^ apart) for i in range(n_vocab * n_data)])  16.6 us
    ppermute x7, starting transfers between devices, from_device(): lax.ppermute(x, AXES, [(i, i ^ apart) for i in range(n_vocab * n_data)])  8.61 us
    all_to_all x1, starting transfers between devices, local(): lax.all_to_all(pack(rows, n_vocab, n_data), AXES, split_axis=0, concat_ax...  7.33 us
    pallas_call x1, Pallas kernels, make_table(): pl.pallas_call(functools.partial(table_kernel, scale, n_vocab, n_data), o...  7.02 us
    pallas_call x1, Pallas kernels, pack(): pl.pallas_call(functools.partial(pack_kernel, n_vocab, n_data), out_shape...  2.03 us
  transfers between devices with their start and end apart: 8, of which 7 were waited for; matrix products, arithmetic and copies ran while one was open for 3% of the time, Pallas kernels for 1%

profile of v9, /device:TPU:0, one launch (start us, length us, event | category | flops | bytes accessed | tf_op | source)
XLA Modules:
  0.0 44.7 jit_solution(7545454863917567282)
XLA Ops:
  0.6 2.0 %pack.1 = bf16[32,128,128]{2,1,0:T(8,128)(2,1)} custom-call(bf16[128,4096]{1,0:T(8,128)(2,1)} %rows_hbm.1), custom_call_target="tpu_custom_call" | custom-call | tf_op jit(solution)/shard_map/pack/pallas_call | solution.py:67
  2.7 7.3 %all-to-all-start = ((bf16[32,128,128]{2,1,0:T(8,128)(2,1)}), bf16[32,128,128]{2,1,0:T(8,128)(2,1)S(1)}, u32[]{:S(2)}, u32[]{:S(2)}) async-start(bf16[32,128,128]{2,1,0:T(8,128)(2,1)} %pack.1), calls=%async_computation | async-start | bytes 2097152 | tf_op jit(solution)/shard_map/all_to_all | solution.py:294
  10.0 0.3 collective-permute-start
  10.3 1.0 %collective-permute-done = s32[1,128]{1,0:T(1,128)S(1)} collective-permute-done((s32[1,128]{1,0:T(1,128)}, s32[1,128]{1,0:T(1,128)S(1)}, u32[]{:S(2)}, u32[]{:S(2)}) %collective-permute-start) | collective-permute-done | bytes 544 | tf_op jit(solution)/shard_map/ppermute | solution.py:84
  11.4 0.7 %pad_add_fusion = s32[2,128]{1,0:T(2,128)S(1)} fusion(s32[1,128]{1,0:T(1,128)S(1)} %collective-permute-done, s32[1,128]{1,0:T(1,128)} %bitcast.4), kind=kLoop, calls=%fused_computation | loop fusion | flops 256 | bytes 2048 | tf_op jit(solution)/shard_map/concatenate | solution.py:86
  12.0 2.7 %collective-permute-start.3 = (s32[2,128]{1,0:T(2,128)S(1)}, s32[2,128]{1,0:T(2,128)S(1)}, u32[]{:S(2)}, u32[]{:S(2)}) collective-permute-start(s32[2,128]{1,0:T(2,128)S(1)} %pad_add_fusion), channel_id=1, source_target_pairs={{0,24},{1,25},{2,26},{3,27},{4,28},{5,29},{6,30},{7,31},{8,16},{9,... | collective-permute-start | bytes 3080 | tf_op jit(solution)/shard_map/ppermute | solution.py:84
  14.7 0.6 %collective-permute-start.2 = (s32[2,128]{1,0:T(2,128)S(1)}, s32[2,128]{1,0:T(2,128)S(1)}, u32[]{:S(2)}, u32[]{:S(2)}) collective-permute-start(s32[2,128]{1,0:T(2,128)S(1)} %pad_add_fusion), channel_id=1, source_target_pairs={{0,16},{1,17},{2,18},{3,19},{4,20},{5,21},{6,22},{7,23},{8,24},{9,... | collective-permute-start | bytes 3080 | tf_op jit(solution)/shard_map/ppermute | solution.py:84
  15.3 0.3 collective-permute-start.1
  15.5 2.7 %collective-permute-done.3 = s32[2,128]{1,0:T(2,128)S(1)} collective-permute-done((s32[2,128]{1,0:T(2,128)S(1)}, s32[2,128]{1,0:T(2,128)S(1)}, u32[]{:S(2)}, u32[]{:S(2)}) %collective-permute-start.3) | collective-permute-done | bytes 1056 | tf_op jit(solution)/shard_map/ppermute | solution.py:84
  18.2 0.1 collective-permute-done.2
  18.3 0.6 %collective-permute-done.1 = s32[2,128]{1,0:T(2,128)S(1)} collective-permute-done((s32[2,128]{1,0:T(2,128)S(1)}, s32[2,128]{1,0:T(2,128)S(1)}, u32[]{:S(2)}, u32[]{:S(2)}) %collective-permute-start.1) | collective-permute-done | bytes 1056 | tf_op jit(solution)/shard_map/ppermute | solution.py:84
  18.9 0.7 %concatenate.8.refs_0_ = s32[8,128]{1,0:T(8,128)S(1)} concatenate(s32[1,128]{1,0:T(1,128)} %bitcast.5, s32[1,128]{1,0:T(1,128)S(1)} %collective-permute-done, s32[2,128]{1,0:T(2,128)S(1)} %collective-permute-done.1, s32[2,128]{1,0:T(2,128)S(1)} %collective-permute-done.2, s32[2,128]{1,0:T(2,128)S(1)} %collective-permute-done.3), dimensions={0} | concatenate | bytes 8192 | tf_op jit(solution)/shard_map/concatenate | solution.py:87
  19.6 4.2 %collective-permute-start.6 = (s32[8,128]{1,0:T(8,128)S(1)}, s32[8,128]{1,0:T(8,128)S(1)}, u32[]{:S(2)}, u32[]{:S(2)}) collective-permute-start(s32[8,128]{1,0:T(8,128)S(1)} %concatenate.8.refs_0_), channel_id=1, source_target_pairs={{0,6},{1,7},{2,4},{3,5},{4,2},{5,3},{6,0},{7,1},{8,14},{9,15},{10,... | collective-permute-start | bytes 12296 | tf_op jit(solution)/shard_map/ppermute | solution.py:84
  23.7 0.0 collective-permute-start.5
  23.7 0.6 %collective-permute-start.4 = (s32[8,128]{1,0:T(8,128)S(1)}, s32[8,128]{1,0:T(8,128)S(1)}, u32[]{:S(2)}, u32[]{:S(2)}) collective-permute-start(s32[8,128]{1,0:T(8,128)S(1)} %concatenate.8.refs_0_), channel_id=1, source_target_pairs={{0,2},{1,3},{2,0},{3,1},{4,6},{5,7},{6,4},{7,5},{8,10},{9,11},{10,... | collective-permute-start | bytes 12296 | tf_op jit(solution)/shard_map/ppermute | solution.py:84
  24.4 7.3 %collective-permute-done.6.refs_3_ = s32[8,128]{1,0:T(8,128)S(1)} collective-permute-done((s32[8,128]{1,0:T(8,128)S(1)}, s32[8,128]{1,0:T(8,128)S(1)}, u32[]{:S(2)}, u32[]{:S(2)}) %collective-permute-start.6) | collective-permute-done | bytes 4128 | tf_op jit(solution)/shard_map/ppermute | solution.py:84
  31.7 4.8 %collective-permute-done.5.refs_2_ = s32[8,128]{1,0:T(8,128)S(1)} collective-permute-done((s32[8,128]{1,0:T(8,128)S(1)}, s32[8,128]{1,0:T(8,128)S(1)}, u32[]{:S(2)}, u32[]{:S(2)}) %collective-permute-start.5) | collective-permute-done | bytes 4128 | tf_op jit(solution)/shard_map/ppermute | solution.py:84
  36.6 0.0 collective-permute-done.4.refs_1_
  36.6 0.6 %place.1.placed = s32[16,128]{1,0:T(8,128)S(1)} custom-call(s32[8,128]{1,0:T(8,128)S(1)} %concatenate.8.refs_0_, s32[8,128]{1,0:T(8,128)S(1)} %collective-permute-done.4.refs_1_, s32[8,128]{1,0:T(8,128)S(1)} %collective-permute-done.5.refs_2_, s32[8,128]{1,0:T(8,128)S(1)} %collective-permute-done.6.refs_3_), custom_call_target="tpu_custom_call" | custom-call | tf_op jit(solution)/shard_map/place/pallas_call | solution.py:134
  37.2 0.5 %all-to-all-done.got = bf16[32,128,128]{2,1,0:T(8,128)(2,1)S(1)} async-done(((bf16[32,128,128]{2,1,0:T(8,128)(2,1)}), bf16[32,128,128]{2,1,0:T(8,128)(2,1)S(1)}, u32[]{:S(2)}, u32[]{:S(2)}) %all-to-all-start) | async-done | bytes 1048608 | tf_op jit(solution)/shard_map/all_to_all | solution.py:294
  37.6 7.0 %table.1 = (f32[8016,512]{1,0:T(8,128)}, f32[64,128]{1,0:T(8,128)}) custom-call(bf16[32,128,128]{2,1,0:T(8,128)(2,1)S(1)} %all-to-all-done.got, s32[16,128]{1,0:T(8,128)S(1)} %place.1.placed), custom_call_target="tpu_custom_call" | custom-call | tf_op jit(solution)/shard_map/table/pallas_call | solution.py:268
Async XLA Ops:
  2.7 35.0 %all-to-all-start = ((bf16[32,128,128]{2,1,0:T(8,128)(2,1)}), bf16[32,128,128]{2,1,0:T(8,128)(2,1)S(1)}, u32[]{:S(2)}, u32[]{:S(2)}) async-start(bf16[32,128,128]{2,1,0:T(8,128)(2,1)} %pack.1), calls=%async_computation | async-start | bytes 2097152 | tf_op jit(solution)/shard_map/all_to_all | solution.py:294
  10.0 1.4 %collective-permute-start = (s32[1,128]{1,0:T(1,128)}, s32[1,128]{1,0:T(1,128)S(1)}, u32[]{:S(2)}, u32[]{:S(2)}) collective-permute-start(s32[1,128]{1,0:T(1,128)} %bitcast.3), channel_id=1, source_target_pairs={{0,1},{1,0},{2,3},{3,2},{4,5},{5,4},{6,7},{7,6},{8,9},{9,8},{10,11... | collective-permute-start | bytes 1544 | tf_op jit(solution)/shard_map/ppermute | solution.py:84
  12.0 6.1 %collective-permute-start.3 = (s32[2,128]{1,0:T(2,128)S(1)}, s32[2,128]{1,0:T(2,128)S(1)}, u32[]{:S(2)}, u32[]{:S(2)}) collective-permute-start(s32[2,128]{1,0:T(2,128)S(1)} %pad_add_fusion), channel_id=1, source_target_pairs={{0,24},{1,25},{2,26},{3,27},{4,28},{5,29},{6,30},{7,31},{8,16},{9,... | collective-permute-start | bytes 3080 | tf_op jit(solution)/shard_map/ppermute | solution.py:84
  14.7 3.6 %collective-permute-start.2 = (s32[2,128]{1,0:T(2,128)S(1)}, s32[2,128]{1,0:T(2,128)S(1)}, u32[]{:S(2)}, u32[]{:S(2)}) collective-permute-start(s32[2,128]{1,0:T(2,128)S(1)} %pad_add_fusion), channel_id=1, source_target_pairs={{0,16},{1,17},{2,18},{3,19},{4,20},{5,21},{6,22},{7,23},{8,24},{9,... | collective-permute-start | bytes 3080 | tf_op jit(solution)/shard_map/ppermute | solution.py:84
  15.3 3.6 %collective-permute-start.1 = (s32[2,128]{1,0:T(2,128)S(1)}, s32[2,128]{1,0:T(2,128)S(1)}, u32[]{:S(2)}, u32[]{:S(2)}) collective-permute-start(s32[2,128]{1,0:T(2,128)S(1)} %pad_add_fusion), channel_id=1, source_target_pairs={{0,8},{1,9},{2,10},{3,11},{4,12},{5,13},{6,14},{7,15},{8,0},{9,1},... | collective-permute-start | bytes 3080 | tf_op jit(solution)/shard_map/ppermute | solution.py:84
  19.6 12.2 %collective-permute-start.6 = (s32[8,128]{1,0:T(8,128)S(1)}, s32[8,128]{1,0:T(8,128)S(1)}, u32[]{:S(2)}, u32[]{:S(2)}) collective-permute-start(s32[8,128]{1,0:T(8,128)S(1)} %concatenate.8.refs_0_), channel_id=1, source_target_pairs={{0,6},{1,7},{2,4},{3,5},{4,2},{5,3},{6,0},{7,1},{8,14},{9,15},{10,... | collective-permute-start | bytes 12296 | tf_op jit(solution)/shard_map/ppermute | solution.py:84
  23.7 12.8 %collective-permute-start.5 = (s32[8,128]{1,0:T(8,128)S(1)}, s32[8,128]{1,0:T(8,128)S(1)}, u32[]{:S(2)}, u32[]{:S(2)}) collective-permute-start(s32[8,128]{1,0:T(8,128)S(1)} %concatenate.8.refs_0_), channel_id=1, source_target_pairs={{0,4},{1,5},{2,6},{3,7},{4,0},{5,1},{6,2},{7,3},{8,12},{9,13},{10,... | collective-permute-start | bytes 12296 | tf_op jit(solution)/shard_map/ppermute | solution.py:84
  23.7 12.8 %collective-permute-start.4 = (s32[8,128]{1,0:T(8,128)S(1)}, s32[8,128]{1,0:T(8,128)S(1)}, u32[]{:S(2)}, u32[]{:S(2)}) collective-permute-start(s32[8,128]{1,0:T(8,128)S(1)} %concatenate.8.refs_0_), channel_id=1, source_target_pairs={{0,2},{1,3},{2,0},{3,1},{4,6},{5,7},{6,4},{7,5},{8,10},{9,11},{10,... | collective-permute-start | bytes 12296 | tf_op jit(solution)/shard_map/ppermute | solution.py:84
